TPU v7x, 256 devices: a whole 4x4x8 slice. The times are simulated.
256 devices in a mesh: rows: 64 (over z, x, core), cols: 4 (over y).
Axes of the slice: x: 4, y: 4, z: 8, core: 2. Of those that a mesh axis runs over, the one named last changes fastest.
Arguments:
- left_features: bfloat16 [2, 768, 512, 256], P(None, 'rows', 'cols'), may hold values from -6 to 6
- right_features: bfloat16 [2, 768, 512, 256], P(None, 'rows', 'cols'), may hold values from -6 to 6
- conv_weight: bfloat16 [3, 3, 256, 256], replicated, may hold values from -0.125 to 0.125
- conv_bias: float32 [256], replicated, may hold values from -3 to 3
Outputs:
- pyramid_out: float32 [2, 768, 512, 480], P(None, 'rows', 'cols')
All inputs are finite; a program needn't handle non-finite values.
Results may differ from a plain program's by a relative error of at most 0.0012.
Values may be sent and summed in bfloat16 or wider, within the bound.
A program may use at most 64 MiB of HBM per device.

v0:
```python
import math

import jax
import jax.numpy as jnp
from jax import lax
from jax.sharding import PartitionSpec as P

DISP = 256
LEVELS = 4


def padded_2(cells, sides, width):
    for axis, dim in sides:
        count = lax.axis_size(axis)
        ends = count - 1
        head = lax.slice_in_dim(cells, 0, width, axis=dim)
        tail = lax.slice_in_dim(cells, cells.shape[dim] - width, cells.shape[dim], axis=dim)
        cells = jnp.concatenate(
            [
                lax.ppermute(tail, axis, [(i, (i + 1) % count) for i in range(ends)]),
                cells,
                lax.ppermute(head, axis, [((i + 1) % count, i) for i in range(ends)]),
            ],
            axis=dim,
        )
    return cells


def shifted(value, axis, steps):
    count = lax.axis_size(axis)
    leading, last = (max(0, -steps), min(count, count - steps))
    return lax.ppermute(value, axis, [(source, source + steps) for source in range(leading, last)])


def encode(padded, conv_weight, conv_bias):
    batch = padded.shape[0]
    height = padded.shape[1] - 2
    breadth = padded.shape[2] - 2
    channels = padded.shape[3]
    total = jnp.zeros((batch * height * breadth, channels), jnp.float32)
    for row_tap in range(3):
        for col_tap in range(3):
            window = padded[:, row_tap : row_tap + height, col_tap : col_tap + breadth].reshape(
                -1, channels
            )
            total = total + jnp.dot(
                window, conv_weight[row_tap, col_tap], preferred_element_type=jnp.float32
            )
    centre = padded[:, 1:-1, 1:-1].reshape(-1, channels).astype(jnp.float32)
    encoded = centre + jax.nn.relu(total + conv_bias)
    return encoded.astype(jnp.bfloat16).reshape(batch, height, breadth, channels)


def pyramid(scores, span_count, level_count, channels):
    queries = scores.shape[-2]
    across = scores.shape[-1]
    leading = scores.shape[:-2]
    skewed = scores[..., 1:].reshape(leading + (-1,))
    skewed = jnp.pad(skewed, [(0, 0)] * len(leading) + [(0, queries)])
    skewed = skewed.reshape(leading + (queries, across))[..., :span_count][..., ::-1]
    volume = skewed * (1.0 / math.sqrt(channels))
    levels = [volume]
    for level in range(1, level_count):
        pooled = volume.reshape(leading + (queries, span_count >> level, 1 << level)).mean(axis=-1)
        levels.append(pooled)
    return jnp.concatenate(levels, axis=-1)


def shards(left_features, right_features, conv_weight, conv_bias):
    batch, height, breadth, channels = left_features.shape
    left_pad, right_pad = (
        padded_2(left_features, (("rows", 1), ("cols", 2)), 1),
        padded_2(right_features, (("rows", 1), ("cols", 2)), 1),
    )
    left_out = encode(left_pad, conv_weight, conv_bias)
    right_out = encode(right_pad, conv_weight, conv_bias)
    pieces = []
    for offset in range(DISP // breadth, 0, -1):
        pieces.append(shifted(right_out, "cols", offset))
    pieces.append(right_out)
    window = jnp.concatenate(pieces, axis=2)
    rows_total = batch * height
    scores = jnp.einsum(
        "rxc,ryc->rxy",
        left_out.reshape(rows_total, breadth, channels),
        window.reshape(rows_total, DISP + breadth, channels),
        preferred_element_type=jnp.float32,
    )
    return pyramid(scores, DISP, LEVELS, channels).reshape(batch, height, breadth, -1)


def solution(mesh):
    return jax.shard_map(
        shards,
        mesh=mesh,
        in_specs=(P(None, "rows", "cols", None), P(None, "rows", "cols", None), P(), P()),
        out_specs=P(None, "rows", "cols", None),
        check_vma=False,
    )
```

profile of v0, /device:TPU:118, one launch (start us, length us, event | category | flops | bytes accessed | tf_op | source)
XLA Modules:
  0.0 144.2 jit_solution(9518510883111668882)
XLA Ops:
  0.0 1.0 fusion.68
  1.0 1.9 %collective-permute-start = (bf16[2,1,128,256]{3,2,1,0:T(8,128)(2,1)S(1)}, bf16[2,1,128,256]{3,2,1,0:T(8,128)(2,1)S(1)}, u32[]{:S(2)}, u32[]{:S(2)}) collective-permute-start(bf16[2,1,128,256]{3,2,1,0:T(8,128)(2,1)S(1)} %get-tuple-element.36), channel_id=1, source_target_pairs={{0,4},{4,8},{8,12},{12,16},{16,20},{20,24},{24,28},{28,32},{32,36}... | collective-permute-start | bytes 393224 | tf_op jit(solution)/shard_map/ppermute | solution.py:20
  2.9 3.6 %collective-permute-start.1 = (bf16[2,1,128,256]{3,2,1,0:T(8,128)(2,1)S(1)}, bf16[2,1,128,256]{3,2,1,0:T(8,128)(2,1)S(1)}, u32[]{:S(2)}, u32[]{:S(2)}) collective-permute-start(bf16[2,1,128,256]{3,2,1,0:T(8,128)(2,1)S(1)} %get-tuple-element.35), channel_id=1, source_target_pairs={{4,0},{8,4},{12,8},{16,12},{20,16},{24,20},{28,24},{32,28},{36,32}... | collective-permute-start | bytes 393224 | tf_op jit(solution)/shard_map/ppermute | solution.py:22
  6.6 1.0 fusion.67
  7.6 3.3 %collective-permute-start.4 = (bf16[2,1,128,256]{3,2,1,0:T(8,128)(2,1)S(1)}, bf16[2,1,128,256]{3,2,1,0:T(8,128)(2,1)S(1)}, u32[]{:S(2)}, u32[]{:S(2)}) collective-permute-start(bf16[2,1,128,256]{3,2,1,0:T(8,128)(2,1)S(1)} %get-tuple-element.31), channel_id=1, source_target_pairs={{0,4},{4,8},{8,12},{12,16},{16,20},{20,24},{24,28},{28,32},{32,36}... | collective-permute-start | bytes 393224 | tf_op jit(solution)/shard_map/ppermute | solution.py:20
  10.9 2.2 %collective-permute-start.5 = (bf16[2,1,128,256]{3,2,1,0:T(8,128)(2,1)S(1)}, bf16[2,1,128,256]{3,2,1,0:T(8,128)(2,1)S(1)}, u32[]{:S(2)}, u32[]{:S(2)}) collective-permute-start(bf16[2,1,128,256]{3,2,1,0:T(8,128)(2,1)S(1)} %get-tuple-element.30), channel_id=1, source_target_pairs={{4,0},{8,4},{12,8},{16,12},{20,16},{24,20},{28,24},{32,28},{36,32}... | collective-permute-start | bytes 393224 | tf_op jit(solution)/shard_map/ppermute | solution.py:22
  13.2 2.8 %pad_maximum_fusion.12 = (bf16[2,12,128,256]{3,2,1,0:T(8,128)(2,1)S(1)}, bf16[2,14,128,256]{3,2,1,0:T(8,128)(2,1)S(1)}, bf16[2,12,128,256]{3,2,1,0:T(8,128)(2,1)S(1)}) fusion(bf16[2,12,128,256]{3,2,1,0:T(8,128)(2,1)} %param.4, bf16[2,1,128,256]{3,2,1,0:T(8,128)(2,1)S(1)} %collective-permute-done, ...), kind=kLoop, calls=%fused_computation.64 | loop fusion | flops 6291456 | bytes 6553600 | tf_op jit(solution)/shard_map/concatenate | solution.py:18
  16.1 3.2 %collective-permute-start.2 = (bf16[2,14,1,256]{3,2,1,0:T(2,128)(2,1)S(1)}, bf16[2,14,1,256]{3,2,1,0:T(2,128)(2,1)S(1)}, u32[]{:S(2)}, u32[]{:S(2)}) collective-permute-start(bf16[2,14,1,256]{3,2,1,0:T(2,128)(2,1)S(1)} %get-tuple-element.25), channel_id=1, source_target_pairs={{0,1},{1,2},{2,3},{4,5},{5,6},{6,7},{8,9},{9,10},{10,11},{12,13},{... | collective-permute-start | bytes 43016 | tf_op jit(solution)/shard_map/ppermute | solution.py:20
  19.3 2.7 %collective-permute-start.3 = (bf16[2,14,1,256]{3,2,1,0:T(2,128)(2,1)S(1)}, bf16[2,14,1,256]{3,2,1,0:T(2,128)(2,1)S(1)}, u32[]{:S(2)}, u32[]{:S(2)}) collective-permute-start(bf16[2,14,1,256]{3,2,1,0:T(2,128)(2,1)S(1)} %get-tuple-element.26), channel_id=1, source_target_pairs={{1,0},{2,1},{3,2},{5,4},{6,5},{7,6},{9,8},{10,9},{11,10},{13,12},{... | collective-permute-start | bytes 43016 | tf_op jit(solution)/shard_map/ppermute | solution.py:22
  24.6 3.2 %collective-permute-start.6 = (bf16[2,14,1,256]{3,2,1,0:T(2,128)(2,1)S(1)}, bf16[2,14,1,256]{3,2,1,0:T(2,128)(2,1)S(1)}, u32[]{:S(2)}, u32[]{:S(2)}) collective-permute-start(bf16[2,14,1,256]{3,2,1,0:T(2,128)(2,1)S(1)} %get-tuple-element.20), channel_id=1, source_target_pairs={{0,1},{1,2},{2,3},{4,5},{5,6},{6,7},{8,9},{9,10},{10,11},{12,13},{... | collective-permute-start | bytes 43016 | tf_op jit(solution)/shard_map/ppermute | solution.py:20
  27.8 2.7 %collective-permute-start.7 = (bf16[2,14,1,256]{3,2,1,0:T(2,128)(2,1)S(1)}, bf16[2,14,1,256]{3,2,1,0:T(2,128)(2,1)S(1)}, u32[]{:S(2)}, u32[]{:S(2)}) collective-permute-start(bf16[2,14,1,256]{3,2,1,0:T(2,128)(2,1)S(1)} %get-tuple-element.21), channel_id=1, source_target_pairs={{1,0},{2,1},{3,2},{5,4},{6,5},{7,6},{9,8},{10,9},{11,10},{13,12},{... | collective-permute-start | bytes 43016 | tf_op jit(solution)/shard_map/ppermute | solution.py:22
  31.6 1.9 %collective-permute-done.7 = bf16[2,14,1,256]{3,2,1,0:T(2,128)(2,1)S(1)} collective-permute-done((bf16[2,14,1,256]{3,2,1,0:T(2,128)(2,1)S(1)}, bf16[2,14,1,256]{3,2,1,0:T(2,128)(2,1)S(1)}, u32[]{:S(2)}, u32[]{:S(2)}) %collective-permute-start.7) | collective-permute-done | bytes 14368 | tf_op jit(solution)/shard_map/ppermute | solution.py:22
  33.5 5.1 %pad_maximum_fusion.7 = (bf16[2,12,128,256]{3,2,1,0:T(8,128)(2,1)S(1)}, bf16[2,12,128,256]{3,2,1,0:T(8,128)(2,1)S(1)}, bf16[2,12,128,256]{3,2,1,0:T(8,128)(2,1)S...) fusion(bf16[2,14,128,256]{3,2,1,0:T(8,128)(2,1)S(1)} %constant_, ...), kind=kLoop, calls=%fused_computation.59 | loop fusion | flops 18874368 | bytes 11300864 | tf_op jit(solution)/shard_map/concatenate | solution.py:18
  42.3 1.2 fusion.12
  43.5 1.9 %collective-permute-start.9 = (bf16[2,12,128,256]{3,2,1,0:T(8,128)(2,1)S(1)}, bf16[2,12,128,256]{3,2,1,0:T(8,128)(2,1)S(1)}, u32[]{:S(2)}, u32[]{:S(2)}) collective-permute-start(bf16[2,12,128,256]{3,2,1,0:T(8,128)(2,1)S(1)} %bitcast.120), channel_id=1, source_target_pairs={{0,1},{1,2},{2,3},{4,5},{5,6},{6,7},{8,9},{9,10},{10,11},{12,13},{... | collective-permute-start | bytes 4718600 | tf_op jit(solution)/shard_map/ppermute | solution.py:32
  45.4 1.5 %collective-permute-start.8 = (bf16[2,12,128,256]{3,2,1,0:T(8,128)(2,1)S(1)}, bf16[2,12,128,256]{3,2,1,0:T(8,128)(2,1)S(1)}, u32[]{:S(2)}, u32[]{:S(2)}) collective-permute-start(bf16[2,12,128,256]{3,2,1,0:T(8,128)(2,1)S(1)} %bitcast.121), channel_id=1, source_target_pairs={{0,2},{1,3},{4,6},{5,7},{8,10},{9,11},{12,14},{13,15},{16,18},{17,... | collective-permute-start | bytes 4718600 | tf_op jit(solution)/shard_map/ppermute | solution.py:32
  46.9 5.1 %pad_maximum_fusion.11 = (bf16[2,12,128,256]{3,2,1,0:T(8,128)(2,1)S(1)}, bf16[2,12,128,256]{3,2,1,0:T(8,128)(2,1)S(1)}, bf16[2,12,128,256]{3,2,1,0:T(8,128)(2,1)...) fusion(bf16[2,14,128,256]{3,2,1,0:T(8,128)(2,1)S(1)} %constant_, ...), kind=kLoop, calls=%fused_computation.63 | loop fusion | flops 18874368 | bytes 11300864 | tf_op jit(solution)/shard_map/concatenate | solution.py:18
  54.4 0.8 copy-done.1
  56.4 1.3 fusion.13
  57.7 23.2 %collective-permute-done.9 = bf16[2,12,128,256]{3,2,1,0:T(8,128)(2,1)S(1)} collective-permute-done((bf16[2,12,128,256]{3,2,1,0:T(8,128)(2,1)S(1)}, bf16[2,12,128,256]{3,2,1,0:T(8,128)(2,1)S(1)}, u32[]{:S(2)}, u32[]{:S(2)}) %collective-permute-start.9) | collective-permute-done | bytes 1572896 | tf_op jit(solution)/shard_map/ppermute | solution.py:32
  80.8 33.9 %collective-permute-done.8 = bf16[2,12,128,256]{3,2,1,0:T(8,128)(2,1)S(1)} collective-permute-done((bf16[2,12,128,256]{3,2,1,0:T(8,128)(2,1)S(1)}, bf16[2,12,128,256]{3,2,1,0:T(8,128)(2,1)S(1)}, u32[]{:S(2)}, u32[]{:S(2)}) %collective-permute-start.8) | collective-permute-done | bytes 1572896 | tf_op jit(solution)/shard_map/ppermute | solution.py:32
  114.7 3.2 %fusion = f32[24,128,383]{2,1,0:T(8,128)} fusion(bf16[24,128,256]{2,1,0:T(8,128)(2,1)S(1)} %bitcast.123, bf16[24,128,256]{2,1,0:T(8,128)(2,1)S(1)} %bitcast.122, bf16[24,128,256]{2,1,0:T(8,128)(2,1)S(1)} %bitcast.124, bf16[24,128,256]{2,1,0:T(8,128)(2,1)S(1)} %bitcast.125), kind=kOutput, calls=%fused_computation.2 | convolution fusion | flops 616525824 | bytes 10997760 | tf_op jit(solution)/shard_map/rxc,ryc->rxy/dot_general | solution.py:83
  117.9 6.6 %reshape.102 = f32[24,49024]{1,0:T(8,128)} reshape(f32[24,128,383]{2,1,0:T(8,128)} %fusion) | data formatting | bytes 9412608 | tf_op jit(solution)/shard_map/reshape | solution.py:58
  124.5 2.6 %pad.4 = f32[24,49152]{1,0:T(8,128)S(1)} pad(f32[24,49024]{1,0:T(8,128)} %reshape.102, f32[]{:T(128)} %constant.6.clone.1), padding=0_0x0_128 | pad | bytes 9424900 | tf_op jit(solution)/shard_map/jit(_pad)/pad | solution.py:59
  127.2 0.8 copy.19
  128.0 2.0 %slice.186 = f32[24,128,256]{2,1,0:T(8,128)} slice(f32[24,128,384]{2,1,0:T(8,128)S(1)} %bitcast.109), slice={[0:24], [0:128], [0:256]} | slice | bytes 6291456 | tf_op jit(solution)/shard_map/slice | solution.py:60
  129.9 2.5 %copy.18 = f32[24,128,256]{1,0,2:T(8,128)S(1)} copy(f32[24,128,256]{2,1,0:T(8,128)} %slice.186) | data formatting | bytes 6291456
  133.4 1.9 %reverse_multiply_fusion = f32[24,128,256]{1,0,2:T(8,128)} fusion(f32[24,128,256]{1,0,2:T(8,128)S(1)} %copy.18), kind=kLoop, calls=%fused_computation.32 | loop fusion | flops 786432 | bytes 6291456 | tf_op jit(solution)/shard_map/mul | solution.py:61
  135.4 1.0 copy.15
  136.4 1.3 broadcast_multiply_fusion
  137.7 2.9 %pad_maximum_fusion = f32[24,128,480]{1,0,2:T(8,128)S(1)} fusion(f32[24,128,32]{1,0,2:T(8,128)} %copy.15, f32[24,128,64]{1,0,2:T(8,128)S(1)} %broadcast_multiply_fusion.1, f32[24,128,128]{1,0,2:T(8,128)} %broadcast_multiply_fusion, f32[24,128,256]{1,0,2:T(8,128)} %reverse_multiply_fusion), kind=kLoop, calls=%fused_computation | loop fusion | flops 4423680 | bytes 11796480 | tf_op jit(solution)/shard_map/concatenate | solution.py:66
  140.6 3.6 %copy.16 = f32[24,128,480]{1,2,0:T(8,128)} copy(f32[24,128,480]{1,0,2:T(8,128)S(1)} %pad_maximum_fusion) | data formatting | bytes 11796480 | tf_op jit(solution)/shard_map/concatenate | solution.py:66
  (42 shorter events, 12.0 us)
Async XLA Ops:
  1.0 12.2 %collective-permute-start = (bf16[2,1,128,256]{3,2,1,0:T(8,128)(2,1)S(1)}, bf16[2,1,128,256]{3,2,1,0:T(8,128)(2,1)S(1)}, u32[]{:S(2)}, u32[]{:S(2)}) collective-permute-start(bf16[2,1,128,256]{3,2,1,0:T(8,128)(2,1)S(1)} %get-tuple-element.36), channel_id=1, source_target_pairs={{0,4},{4,8},{8,12},{12,16},{16,20},{20,24},{24,28},{28,32},{32,36}... | collective-permute-start | bytes 393224 | tf_op jit(solution)/shard_map/ppermute | solution.py:20
  2.9 10.3 %collective-permute-start.1 = (bf16[2,1,128,256]{3,2,1,0:T(8,128)(2,1)S(1)}, bf16[2,1,128,256]{3,2,1,0:T(8,128)(2,1)S(1)}, u32[]{:S(2)}, u32[]{:S(2)}) collective-permute-start(bf16[2,1,128,256]{3,2,1,0:T(8,128)(2,1)S(1)} %get-tuple-element.35), channel_id=1, source_target_pairs={{4,0},{8,4},{12,8},{16,12},{20,16},{24,20},{28,24},{32,28},{36,32}... | collective-permute-start | bytes 393224 | tf_op jit(solution)/shard_map/ppermute | solution.py:22
  7.6 15.5 %collective-permute-start.4 = (bf16[2,1,128,256]{3,2,1,0:T(8,128)(2,1)S(1)}, bf16[2,1,128,256]{3,2,1,0:T(8,128)(2,1)S(1)}, u32[]{:S(2)}, u32[]{:S(2)}) collective-permute-start(bf16[2,1,128,256]{3,2,1,0:T(8,128)(2,1)S(1)} %get-tuple-element.31), channel_id=1, source_target_pairs={{0,4},{4,8},{8,12},{12,16},{16,20},{20,24},{24,28},{28,32},{32,36}... | collective-permute-start | bytes 393224 | tf_op jit(solution)/shard_map/ppermute | solution.py:20
  10.9 12.2 %collective-permute-start.5 = (bf16[2,1,128,256]{3,2,1,0:T(8,128)(2,1)S(1)}, bf16[2,1,128,256]{3,2,1,0:T(8,128)(2,1)S(1)}, u32[]{:S(2)}, u32[]{:S(2)}) collective-permute-start(bf16[2,1,128,256]{3,2,1,0:T(8,128)(2,1)S(1)} %get-tuple-element.30), channel_id=1, source_target_pairs={{4,0},{8,4},{12,8},{16,12},{20,16},{24,20},{28,24},{32,28},{36,32}... | collective-permute-start | bytes 393224 | tf_op jit(solution)/shard_map/ppermute | solution.py:22
  13.2 8.7 %copy-start.2 = (bf16[3,3,256,256]{3,2,1,0:T(8,128)(2,1)S(1)}, bf16[3,3,256,256]{3,2,1,0:T(8,128)(2,1)}, u32[]{:S(2)}) copy-start(bf16[3,3,256,256]{3,2,1,0:T(8,128)(2,1)} %param.6) | copy-start | bytes 3538948
  16.1 30.8 %collective-permute-start.2 = (bf16[2,14,1,256]{3,2,1,0:T(2,128)(2,1)S(1)}, bf16[2,14,1,256]{3,2,1,0:T(2,128)(2,1)S(1)}, u32[]{:S(2)}, u32[]{:S(2)}) collective-permute-start(bf16[2,14,1,256]{3,2,1,0:T(2,128)(2,1)S(1)} %get-tuple-element.25), channel_id=1, source_target_pairs={{0,1},{1,2},{2,3},{4,5},{5,6},{6,7},{8,9},{9,10},{10,11},{12,13},{... | collective-permute-start | bytes 43016 | tf_op jit(solution)/shard_map/ppermute | solution.py:20
  19.3 27.6 %collective-permute-start.3 = (bf16[2,14,1,256]{3,2,1,0:T(2,128)(2,1)S(1)}, bf16[2,14,1,256]{3,2,1,0:T(2,128)(2,1)S(1)}, u32[]{:S(2)}, u32[]{:S(2)}) collective-permute-start(bf16[2,14,1,256]{3,2,1,0:T(2,128)(2,1)S(1)} %get-tuple-element.26), channel_id=1, source_target_pairs={{1,0},{2,1},{3,2},{5,4},{6,5},{7,6},{9,8},{10,9},{11,10},{13,12},{... | collective-permute-start | bytes 43016 | tf_op jit(solution)/shard_map/ppermute | solution.py:22
  22.5 1.4 copy-start
  24.6 7.0 %collective-permute-start.6 = (bf16[2,14,1,256]{3,2,1,0:T(2,128)(2,1)S(1)}, bf16[2,14,1,256]{3,2,1,0:T(2,128)(2,1)S(1)}, u32[]{:S(2)}, u32[]{:S(2)}) collective-permute-start(bf16[2,14,1,256]{3,2,1,0:T(2,128)(2,1)S(1)} %get-tuple-element.20), channel_id=1, source_target_pairs={{0,1},{1,2},{2,3},{4,5},{5,6},{6,7},{8,9},{9,10},{10,11},{12,13},{... | collective-permute-start | bytes 43016 | tf_op jit(solution)/shard_map/ppermute | solution.py:20
  27.8 5.8 %collective-permute-start.7 = (bf16[2,14,1,256]{3,2,1,0:T(2,128)(2,1)S(1)}, bf16[2,14,1,256]{3,2,1,0:T(2,128)(2,1)S(1)}, u32[]{:S(2)}, u32[]{:S(2)}) collective-permute-start(bf16[2,14,1,256]{3,2,1,0:T(2,128)(2,1)S(1)} %get-tuple-element.21), channel_id=1, source_target_pairs={{1,0},{2,1},{3,2},{5,4},{6,5},{7,6},{9,8},{10,9},{11,10},{13,12},{... | collective-permute-start | bytes 43016 | tf_op jit(solution)/shard_map/ppermute | solution.py:22
  41.6 0.7 copy-start.3
  43.5 37.4 %collective-permute-start.9 = (bf16[2,12,128,256]{3,2,1,0:T(8,128)(2,1)S(1)}, bf16[2,12,128,256]{3,2,1,0:T(8,128)(2,1)S(1)}, u32[]{:S(2)}, u32[]{:S(2)}) collective-permute-start(bf16[2,12,128,256]{3,2,1,0:T(8,128)(2,1)S(1)} %bitcast.120), channel_id=1, source_target_pairs={{0,1},{1,2},{2,3},{4,5},{5,6},{6,7},{8,9},{9,10},{10,11},{12,13},{... | collective-permute-start | bytes 4718600 | tf_op jit(solution)/shard_map/ppermute | solution.py:32
  45.4 69.3 %collective-permute-start.8 = (bf16[2,12,128,256]{3,2,1,0:T(8,128)(2,1)S(1)}, bf16[2,12,128,256]{3,2,1,0:T(8,128)(2,1)S(1)}, u32[]{:S(2)}, u32[]{:S(2)}) collective-permute-start(bf16[2,12,128,256]{3,2,1,0:T(8,128)(2,1)S(1)} %bitcast.121), channel_id=1, source_target_pairs={{0,2},{1,3},{4,6},{5,7},{8,10},{9,11},{12,14},{13,15},{16,18},{17,... | collective-permute-start | bytes 4718600 | tf_op jit(solution)/shard_map/ppermute | solution.py:32
  53.8 1.4 copy-start.1
where the time goes:
time: 147 us; the launch traced here: 144 us
  waiting for transfers between devices  59 us (40%)
  starting transfers between devices  26.2 us (18%)
  local copies, waits for them, and re-layouts  23 us (16%)
  other arithmetic  20.7 us (14%)
  matrix products  14.9 us (10%)
    ppermute x2, waiting for transfers between devices, shifted(): lax.ppermute(value, axis, [(source, source + steps) for source in range(l...  57 us
    concatenate x4, other arithmetic, padded_2(): jnp.concatenate([lax.ppermute(tail, axis, [(i, (i + 1) % count) for i in...  13.6 us
    dot_general x18, matrix products, encode(): jnp.dot(window, conv_weight[row_tap, col_tap], preferred_element_type=jnp...  11.8 us
    ppermute x4, starting transfers between devices, padded_2(): lax.ppermute(tail, axis, [(i, (i + 1) % count) for i in range(ends)])  11.6 us
    ppermute x4, starting transfers between devices, padded_2(): lax.ppermute(head, axis, [((i + 1) % count, i) for i in range(ends)])  11.2 us
    reshape x1, local copies, waits for them, and re-layouts, pyramid(): skewed = scores[..., 1:].reshape(leading + (-1,))  6.63 us
    unnamed x12, local copies, waits for them, and re-layouts  5.06 us
    concatenate x1, local copies, waits for them, and re-layouts, pyramid(): return jnp.concatenate(levels, axis=-1)  3.64 us
  transfers between devices with their start and end apart: 10, of which 3 were waited for; matrix products, arithmetic and copies ran while one was open for 18% of the time, Pallas kernels for 0%

commit v1 on v0

v1 whole, which is shorter than its diff:
```python
import functools
import math

import jax
import jax.numpy as jnp
from jax import lax
from jax.experimental import pallas as pl
from jax.experimental.pallas import tpu as pltpu
from jax.sharding import PartitionSpec as P

DISP = 256
LEVELS = 4
MESH = pl.DeviceIdType.MESH
F32 = jnp.float32
BF16 = jnp.bfloat16

DIRECT = 2


def kernel(
    rows_total,
    left_hbm,
    right_hbm,
    weight_hbm,
    bias_ref,
    out_hbm,
    buf,
    weight,
    taps,
    enc,
    got,
    result,
    pool,
    flip,
    edge32,
    edge,
    halo,
    corner32,
    corner,
    halo_corner,
    extra,
    load_sem,
    weight_sem,
    row_send,
    row_recv,
    col_send,
    col_recv,
    corner_send,
    corner_recv,
    own_send,
    relay_send,
    got_recv,
    out_sem,
):
    r = lax.axis_index("rows")
    c = lax.axis_index("cols")
    last = rows_total - 1
    batch, height, width, channels = left_hbm.shape
    images = (right_hbm, left_hbm)
    rows = batch * height
    inner = (height - 2) // 2
    chunks = rows // 2

    def place(j):
        is_inner = j < batch * inner
        b = jnp.where(is_inner, j // inner, j - batch * inner)
        first = jnp.where(is_inner, 1 + 2 * (j % inner), 0)
        second = jnp.where(is_inner, 2 + 2 * (j % inner), height - 1)
        return b, first, second

    def place_row(k):
        b, first, second = place(k // 2)
        return b, jnp.where(k % 2 == 0, first, second)

    def load(image, b):
        return pltpu.make_async_copy(
            images[image].at[b], buf.at[image, b, pl.ds(1, height)], load_sem.at[image, b]
        )

    weight_copy = pltpu.make_async_copy(weight_hbm, weight, weight_sem)
    for b in range(batch):
        load(0, b).start()
    weight_copy.start()
    for b in range(batch):
        load(1, b).start()

    barrier = pltpu.get_barrier_semaphore()
    for step in (1, 3):
        pl.semaphore_signal(
            barrier, inc=1, device_id={"rows": r, "cols": (c + step) % 4}, device_id_type=MESH
        )

    @pl.when(r > 0)
    def _():
        pl.semaphore_signal(barrier, inc=1, device_id={"rows": r - 1, "cols": c}, device_id_type=MESH)

    @pl.when(r < last)
    def _():
        pl.semaphore_signal(barrier, inc=1, device_id={"rows": r + 1, "cols": c}, device_id_type=MESH)

    d = lax.broadcasted_iota(jnp.int32, (2 * DISP, DISP - (DISP >> 3)), 0) % DISP
    lane = lax.broadcasted_iota(jnp.int32, (2 * DISP, DISP - (DISP >> 3)), 1)
    table = jnp.zeros(d.shape, F32)
    start = 0
    for level in range(1, LEVELS):
        size = DISP >> level
        inside = jnp.logical_and(lane >= start, lane < start + size)
        hit = jnp.logical_and(inside, (d >> level) == lane - start)
        table = jnp.where(hit, 1.0 / (1 << level), table)
        start += size
    pool[...] = table.astype(BF16)
    i0 = lax.broadcasted_iota(jnp.int32, (width, width), 0)
    i1 = lax.broadcasted_iota(jnp.int32, (width, width), 1)
    flip[...] = jnp.where(i0 + i1 == width - 1, 1.0, 0.0).astype(BF16)

    @pl.when(r == 0)
    def _():
        buf[:, :, 0] = jnp.zeros((2, batch, width, channels), BF16)

    @pl.when(r == last)
    def _():
        buf[:, :, height + 1] = jnp.zeros((2, batch, width, channels), BF16)

    @pl.when(c == 0)
    def _():
        halo[0] = jnp.zeros(halo.shape[1:], BF16)
        halo_corner[0] = jnp.zeros(halo_corner.shape[1:], BF16)

    @pl.when(c == 3)
    def _():
        halo[1] = jnp.zeros(halo.shape[1:], BF16)
        halo_corner[1] = jnp.zeros(halo_corner.shape[1:], BF16)

    def take_column(image, b, row, side):
        if side == 0:
            return buf[image, b, row, width - 16 : width, :].astype(F32)[15:16]
        return buf[image, b, row, 0:16, :].astype(F32)[0:1]

    def extract(image):
        for b in range(batch):
            load(image, b).wait()
        for side in range(2):
            for b in range(batch):
                for h in range(height):
                    edge32[side, b, h + 1 : h + 2, :] = take_column(image, b, h + 1, side)
            edge[side, image] = edge32[side].astype(BF16)

    def column_copy(side, image):
        return pltpu.make_async_remote_copy(
            src_ref=edge.at[side, image],
            dst_ref=halo.at[side, image],
            send_sem=col_send.at[side, image],
            recv_sem=col_recv.at[side, image],
            device_id={"rows": r, "cols": (c + (1 if side == 0 else 3)) % 4},
            device_id_type=MESH,
        )

    def row_copy(side, image, b):
        source, target, to = (height - 1, 0, r + 1) if side == 0 else (0, height + 1, r - 1)
        return pltpu.make_async_remote_copy(
            src_ref=images[image].at[b, source],
            dst_ref=buf.at[image, b, target],
            send_sem=row_send.at[side, image, b],
            recv_sem=row_recv.at[side, image, b],
            device_id={"rows": to, "cols": c},
            device_id_type=MESH,
        )

    def corner_copy(side):
        return pltpu.make_async_remote_copy(
            src_ref=corner.at[side],
            dst_ref=halo_corner.at[side],
            send_sem=corner_send.at[side],
            recv_sem=corner_recv.at[side],
            device_id={"rows": r, "cols": (c + (1 if side == 0 else 3)) % 4},
            device_id_type=MESH,
        )

    sends_col = (c < 3, c > 0)
    gets_col = (c > 0, c < 3)
    sends_row = (r < last, r > 0)
    gets_row = (r > 0, r < last)

    def each_col(conditions, action):
        for side in range(2):
            @pl.when(conditions[side])
            def _(side=side):
                action(side)

    def each_row(conditions, action):
        for side in range(2):
            @pl.when(conditions[side])
            def _(side=side):
                for image in range(2):
                    for b in range(batch):
                        action(side, image, b)

    extract(0)
    neighbours = 2 + (r > 0).astype(jnp.int32) + (r < last).astype(jnp.int32)
    pl.semaphore_wait(barrier, neighbours)
    each_col(sends_col, lambda side: column_copy(side, 0).start())
    each_row(sends_row, lambda side, image, b: row_copy(side, image, b).start())
    extract(1)
    each_col(sends_col, lambda side: column_copy(side, 1).start())

    def product(image, j, slot):
        b, first, second = place(j)
        parts = [
            jnp.concatenate([buf[image, b, first + tap], buf[image, b, second + tap]], axis=0)
            for tap in range(3)
        ]
        window = jnp.concatenate(parts, axis=1)
        for tap in range(3):
            matrix = weight[:, tap].reshape(3 * channels, channels)
            taps[slot, tap] = jnp.dot(window, matrix, preferred_element_type=F32)

    def from_halo(image):
        each_col(gets_col, lambda side: column_copy(side, image).wait_recv())
        for side in range(2):
            vectors = halo[side, image].reshape(batch * 16, channels)
            for tap in range(3):
                extra[side, tap, image] = jnp.dot(
                    vectors, weight[tap, 2 * side], preferred_element_type=F32
                )

    def corners_out():
        each_row(gets_row, lambda side, image, b: row_copy(side, image, b).wait_recv())
        for side in range(2):
            for image in range(2):
                for b in range(batch):
                    for end in range(2):
                        at = (image * batch + b) * 2 + end
                        corner32[side, at : at + 1, :] = take_column(image, b, end * (height + 1), side)
            corner[side] = corner32[side].astype(BF16)
        each_col(sends_col, lambda side: corner_copy(side).start())

    def corners_add(image):
        for side in range(2):
            for end in range(2):
                values = jnp.dot(
                    halo_corner[side], weight[2 * end, 2 * side], preferred_element_type=F32
                )
                for b in range(batch):
                    at = (image * batch + b) * 2 + end
                    to = b * 16 + end * (height + 1)
                    extra[side, 2 * end, image, to : to + 1, :] = values[at : at + 1]

    def corners_in():
        each_col(gets_col, lambda side: corner_copy(side).wait_recv())
        corners_add(0)

    column = lax.broadcasted_iota(jnp.int32, (width, channels), 0)

    def encoded(image, b, h, slot, half):
        span = pl.ds(half * width, width)
        sides = [
            sum(extra[side, tap, image, pl.ds(b * 16 + h + tap, 1), :] for tap in range(3))
            for side in range(2)
        ]
        before = pltpu.roll(taps[slot, 0, span, :], 1, 0)
        after = pltpu.roll(taps[slot, 2, span, :], width - 1, 0)
        total = jnp.where(column == 0, sides[0], before) + taps[slot, 1, span, :]
        total = total + jnp.where(column == width - 1, sides[1], after) + bias_ref[...]
        return (buf[image, b, h + 1].astype(F32) + jnp.maximum(total, 0.0)).astype(BF16)

    def own_copy(k, f):
        direct = k < DIRECT
        to = jnp.where(c == 0, 1, jnp.where(c == 1, jnp.where(direct, 2, 0), 3))
        return pltpu.make_async_remote_copy(
            src_ref=enc.at[0, f],
            dst_ref=got.at[0, f],
            send_sem=own_send.at[f],
            recv_sem=got_recv.at[0, f],
            device_id={"rows": r, "cols": to},
            device_id_type=MESH,
        )

    def relay_copy(f):
        source = jnp.where(c == 3, 1, 0)
        to = jnp.where(c == 0, 3, jnp.where(c == 2, 3, 2))
        return pltpu.make_async_remote_copy(
            src_ref=got.at[source, f],
            dst_ref=got.at[jnp.where(c == 3, 0, 1), f],
            send_sem=relay_send.at[f],
            recv_sem=got_recv.at[jnp.where(c == 3, 0, 1), f],
            device_id={"rows": r, "cols": to},
            device_id_type=MESH,
        )

    def arrival(which, f):
        return pltpu.make_async_remote_copy(
            src_ref=got.at[which, f],
            dst_ref=got.at[which, f],
            send_sem=relay_send.at[f],
            recv_sem=got_recv.at[which, f],
            device_id={"rows": r, "cols": (c + 1) % 4},
            device_id_type=MESH,
        )

    def relays(k):
        direct = k < DIRECT
        return jnp.logical_or(
            c == 1,
            jnp.logical_or(
                jnp.logical_and(c == 2, direct),
                jnp.logical_and(jnp.logical_or(c == 0, c == 3), jnp.logical_not(direct)),
            ),
        )

    def relay(k):
        b, h = place_row(k)
        f = b * height + h

        @pl.when(relays(k))
        def _():
            arrival(jnp.where(c == 3, 1, 0), f).wait_recv()
            relay_copy(f).start()

    def correlate(k):
        b, h = place_row(k)
        f = b * height + h
        direct = k < DIRECT

        @pl.when(jnp.logical_or(c == 3, jnp.logical_and(c == 2, jnp.logical_not(direct))))
        def _():
            arrival(0, f).wait_recv()

        @pl.when(jnp.logical_or(c == 2, jnp.logical_and(c == 3, direct)))
        def _():
            arrival(1, f).wait_recv()

        query = enc[1, f]
        blocks = []
        for distance, keys in enumerate((enc[0, f], got[0, f], got[1, f])):
            scores = lax.dot_general(
                query, keys, (((1,), (1,)), ((), ())), preferred_element_type=F32
            )
            if distance:
                scores = jnp.where(c >= distance, scores, 0.0)
            blocks.append(pltpu.roll(scores, 1, 1, stride=1, stride_axis=0))
        lower = i1 <= i0
        volume = jnp.concatenate(
            [jnp.where(lower, blocks[0], blocks[1]), jnp.where(lower, blocks[1], blocks[2])], axis=1
        ) * (1.0 / math.sqrt(channels))
        high = volume.astype(BF16)
        low = (volume - high.astype(F32)).astype(BF16)
        result[f, :, 0:DISP] = volume
        result[f, :, DISP:] = jnp.dot(
            jnp.concatenate([high, low], axis=1), pool[...], preferred_element_type=F32
        )
        pltpu.make_async_copy(result.at[f], out_hbm.at[b, h], out_sem.at[f]).start()

    weight_copy.wait()
    product(0, 0, 0)
    from_halo(0)

    def right_chunk(j, _):
        slot = j % 2

        @pl.when(j == 6)
        def _():
            corners_out()

        @pl.when(j == 9)
        def _():
            corners_in()

        following = j + 1
        product_image = following // chunks
        product(product_image, following % chunks, 1 - slot)
        b, first, second = place(j)
        for half, h in enumerate((first, second)):
            value = encoded(0, b, h, slot, half)
            f = b * height + h
            enc[0, f] = jnp.dot(flip[...], value, preferred_element_type=F32).astype(BF16)

        @pl.when(c < 3)
        def _():
            own_copy(2 * j, b * height + first).start()
            own_copy(2 * j + 1, b * height + second).start()

        @pl.when(j == 8)
        def _():
            relay(0)

        @pl.when(j == 11)
        def _():
            relay(1)

        return 0

    lax.fori_loop(0, chunks, right_chunk, 0)
    from_halo(1)
    corners_add(1)

    early = 6

    def left_chunk(j, _):
        slot = (chunks + j) % 2
        product(1, jnp.minimum(j + 1, chunks - 1), 1 - slot)
        b, first, second = place(j)
        for half, h in enumerate((first, second)):
            enc[1, b * height + h] = encoded(1, b, h, slot, half)

        @pl.when(j % 3 == 2)
        def _():
            relay(2 + j // 3)

        return 0

    lax.fori_loop(0, chunks, left_chunk, 0)

    def score_row(k, _):
        @pl.when(k + early < rows)
        def _():
            relay(k + early)

        correlate(k)
        return 0

    lax.fori_loop(0, rows, score_row, 0)

    def drain(k, _):
        b, h = place_row(k)
        f = b * height + h
        pltpu.make_async_copy(result.at[f], out_hbm.at[b, h], out_sem.at[f]).wait()

        @pl.when(c < 3)
        def _():
            own_copy(k, f).wait_send()

        @pl.when(relays(k))
        def _():
            relay_copy(f).wait_send()

        return 0

    each_col(sends_col, lambda side: column_copy(side, 0).wait_send())
    each_col(sends_col, lambda side: column_copy(side, 1).wait_send())
    each_col(sends_col, lambda side: corner_copy(side).wait_send())
    each_row(sends_row, lambda side, image, b: row_copy(side, image, b).wait_send())
    lax.fori_loop(0, rows, drain, 0)


def shards(rows_total, left_features, right_features, conv_weight, conv_bias):
    batch, height, width, channels = left_features.shape
    rows = batch * height
    lanes = sum(DISP >> level for level in range(LEVELS))
    anywhere = pl.BlockSpec(memory_space=pl.ANY)
    dma = pltpu.SemaphoreType.DMA
    return pl.pallas_call(
        functools.partial(kernel, rows_total),
        out_shape=jax.ShapeDtypeStruct((batch, height, width, lanes), F32),
        in_specs=[anywhere, anywhere, anywhere, pl.BlockSpec(memory_space=pltpu.VMEM)],
        out_specs=anywhere,
        scratch_shapes=[
            pltpu.VMEM((2, batch, height + 2, width, channels), BF16),
            pltpu.VMEM((3, 3, channels, channels), BF16),
            pltpu.VMEM((2, 3, 2 * width, channels), F32),
            pltpu.VMEM((2, rows, width, channels), BF16),
            pltpu.VMEM((2, rows, width, channels), BF16),
            pltpu.VMEM((rows, width, lanes), F32),
            pltpu.VMEM((2 * DISP, lanes - DISP), BF16),
            pltpu.VMEM((width, width), BF16),
            pltpu.VMEM((2, batch, 16, channels), F32),
            pltpu.VMEM((2, 2, batch, 16, channels), BF16),
            pltpu.VMEM((2, 2, batch, 16, channels), BF16),
            pltpu.VMEM((2, 16, channels), F32),
            pltpu.VMEM((2, 16, channels), BF16),
            pltpu.VMEM((2, 16, channels), BF16),
            pltpu.VMEM((2, 3, 2, batch * 16, channels), F32),
            dma((2, batch)),
            dma,
            dma((2, 2, batch)),
            dma((2, 2, batch)),
            dma((2, 2)),
            dma((2, 2)),
            dma((2,)),
            dma((2,)),
            dma((rows,)),
            dma((rows,)),
            dma((2, rows)),
            dma((rows,)),
        ],
        compiler_params=pltpu.CompilerParams(
            collective_id=0, has_side_effects=True, vmem_limit_bytes=40 * 1024 * 1024
        ),
    )(left_features, right_features, conv_weight, conv_bias.reshape(1, channels))


def solution(mesh):
    return jax.shard_map(
        functools.partial(shards, mesh.shape["rows"]),
        mesh=mesh,
        in_specs=(P(None, "rows", "cols", None), P(None, "rows", "cols", None), P(), P()),
        out_specs=P(None, "rows", "cols", None),
        check_vma=False,
    )
```

time: 147 us -> 86.2 us (0.59); the launches traced: 144 us -> 84.9 us
  Pallas kernels: 0 us -> 71.1 us
  waiting for transfers between devices: 59 us -> 0 us
  starting transfers between devices: 26.2 us -> 0 us
  other arithmetic: 20.7 us -> 0 us
  matrix products: 14.9 us -> 0 us
  local copies, waits for them, and re-layouts: 23 us -> 13.8 us
    pallas_call x0 -> x1, Pallas kernels: none -> 71.1 us  [shards(): pl.pallas_call(functools.partial(kernel, rows_total), out_shape=jax.Shape...]
    ppermute x10 -> x0, waiting for transfers between devices: 59 us -> none  [the longest x2 57 us: shifted(): lax.ppermute(value, axis, [(source, source + steps) for source in range(l...]
    ppermute x10 -> x0, starting transfers between devices: 26.2 us -> none  [the longest x4 11.6 us: padded_2(): lax.ppermute(tail, axis, [(i, (i + 1) % count) for i in range(ends)])]
    concatenate x5 -> x0, other arithmetic: 16.5 us -> none  [the longest x4 13.6 us: padded_2(): jnp.concatenate([lax.ppermute(tail, axis, [(i, (i + 1) % count) for i in...]
    dot_general x19 -> x0, matrix products: 14.9 us -> none  [the longest x18 11.8 us: encode(): jnp.dot(window, conv_weight[row_tap, col_tap], preferred_element_type=jnp...]
    reshape x1 -> x0, local copies, waits for them, and re-layouts: 6.63 us -> none  [pyramid(): skewed = scores[..., 1:].reshape(leading + (-1,))]
    pallas_call x0 -> x1, local copies, waits for them, and re-layouts: none -> 6.42 us  [shards(): pl.pallas_call(functools.partial(kernel, rows_total), out_shape=jax.Shape...]
    slice x5 -> x0, local copies, waits for them, and re-layouts: 4.03 us -> none  [the longest x2 1.98 us: padded_2(): head = lax.slice_in_dim(cells, 0, width, axis=dim)]
  transfers between devices with their start and end apart: 10 -> 0, of which waited for: 3 -> 0; matrix products, arithmetic and copies ran while one was open for 18% -> 0% of each run, Pallas kernels for 0% -> 0%
where the time goes in v1:
time: 86.2 us; the launch traced here: 84.9 us
  Pallas kernels  71.1 us (82%)
  local copies, waits for them, and re-layouts  13.8 us (16%)
    pallas_call x1, Pallas kernels, shards(): pl.pallas_call(functools.partial(kernel, rows_total), out_shape=jax.Shape...  71.1 us
    unnamed x10, local copies, waits for them, and re-layouts  7.41 us
    pallas_call x1, local copies, waits for them, and re-layouts, shards(): pl.pallas_call(functools.partial(kernel, rows_total), out_shape=jax.Shape...  6.42 us

profile of v1, /device:TPU:118, one launch (start us, length us, event | category | flops | bytes accessed | tf_op | source)
XLA Modules:
  0.0 84.9 jit_solution(9816104378443917283)
XLA Ops:
  0.0 0.0 copy-start.1
  0.0 1.4 %copy-done.1 = bf16[2,12,128,256]{3,2,1,0:T(8,128)(2,1)S(1)} copy-done((bf16[2,12,128,256]{3,2,1,0:T(8,128)(2,1)S(1)}, bf16[2,12,128,256]{3,2,1,0:T(8,128)(2,1)}, u32[]{:S(2)}) %copy-start.1) | copy-done | bytes 1572888
  1.4 0.0 copy-start.2
  1.4 1.4 %copy-done.2 = bf16[2,12,128,256]{3,2,1,0:T(8,128)(2,1)S(1)} copy-done((bf16[2,12,128,256]{3,2,1,0:T(8,128)(2,1)S(1)}, bf16[2,12,128,256]{3,2,1,0:T(8,128)(2,1)}, u32[]{:S(2)}) %copy-start.2) | copy-done | bytes 1572888
  2.8 0.0 copy-start.3
  2.8 1.3 %copy-done.3 = bf16[3,3,256,256]{3,2,1,0:T(8,128)(2,1)S(1)} copy-done((bf16[3,3,256,256]{3,2,1,0:T(8,128)(2,1)S(1)}, bf16[3,3,256,256]{3,2,1,0:T(8,128)(2,1)}, u32[]{:S(2)}) %copy-start.3) | copy-done | bytes 1179672
  4.1 0.0 copy-start.4
  4.1 0.7 copy-done.4
  4.8 71.1 %shard_map.46 = f32[2,12,128,480]{3,2,1,0:T(8,128)S(1)} custom-call(bf16[2,12,128,256]{3,2,1,0:T(8,128)(2,1)S(1)} %copy-done.1, bf16[2,12,128,256]{3,2,1,0:T(8,128)(2,1)S(1)} %copy-done.2, bf16[3,3,256,256]{3,2,1,0:T(8,128)(2,1)S(1)} %copy-done.3, f32[1,256]{1,0:T(1,128)S(1)} %bitcast.1), custom_call_target="tpu_custom_call" | custom-call | tf_op jit(solution)/shard_map/pallas_call | solution.py:451
  75.9 0.0 copy-start
  75.9 2.6 %copy-done = f32[2,12,128,480]{3,2,1,0:T(8,128)} copy-done((f32[2,12,128,480]{3,2,1,0:T(8,128)}, f32[2,12,128,480]{3,2,1,0:T(8,128)S(1)}, u32[]{:S(2)}) %copy-start) | copy-done | bytes 5898264
  78.5 6.4 %copy.5 = f32[2,12,128,480]{2,3,1,0:T(8,128)} copy(f32[2,12,128,480]{3,2,1,0:T(8,128)} %copy-done) | data formatting | bytes 11796480 | tf_op jit(solution)/shard_map/pallas_call | solution.py:451
Async XLA Ops:
  0.0 1.4 %copy-start.1 = (bf16[2,12,128,256]{3,2,1,0:T(8,128)(2,1)S(1)}, bf16[2,12,128,256]{3,2,1,0:T(8,128)(2,1)}, u32[]{:S(2)}) copy-start(bf16[2,12,128,256]{3,2,1,0:T(8,128)(2,1)} %left_hbm.1) | copy-start | bytes 4718596
  1.4 1.4 %copy-start.2 = (bf16[2,12,128,256]{3,2,1,0:T(8,128)(2,1)S(1)}, bf16[2,12,128,256]{3,2,1,0:T(8,128)(2,1)}, u32[]{:S(2)}) copy-start(bf16[2,12,128,256]{3,2,1,0:T(8,128)(2,1)} %right_hbm.1) | copy-start | bytes 4718596
  2.8 1.3 %copy-start.3 = (bf16[3,3,256,256]{3,2,1,0:T(8,128)(2,1)S(1)}, bf16[3,3,256,256]{3,2,1,0:T(8,128)(2,1)}, u32[]{:S(2)}) copy-start(bf16[3,3,256,256]{3,2,1,0:T(8,128)(2,1)} %weight_hbm.1) | copy-start | bytes 3538948
  4.1 0.7 copy-start.4
  75.9 2.7 %copy-start = (f32[2,12,128,480]{3,2,1,0:T(8,128)}, f32[2,12,128,480]{3,2,1,0:T(8,128)S(1)}, u32[]{:S(2)}) copy-start(f32[2,12,128,480]{3,2,1,0:T(8,128)S(1)} %shard_map.46) | copy-start | bytes 17694724

commit v2 on v1

--- a/solution.py
+++ b/solution.py
@@ -15,6 +15,7 @@
 BF16 = jnp.bfloat16
 
 DIRECT = 2
+LAG = 3
 
 
 def kernel(
@@ -22,14 +23,14 @@
     left_hbm,
     right_hbm,
     weight_hbm,
-    bias_ref,
-    out_hbm,
+    bias_hbm,
+    result,
     buf,
     weight,
+    bias,
     taps,
     enc,
     got,
-    result,
     pool,
     flip,
     edge32,
@@ -41,6 +42,7 @@
     extra,
     load_sem,
     weight_sem,
+    bias_sem,
     row_send,
     row_recv,
     col_send,
@@ -50,7 +52,6 @@
     own_send,
     relay_send,
     got_recv,
-    out_sem,
 ):
     r = lax.axis_index("rows")
     c = lax.axis_index("cols")
@@ -78,28 +79,39 @@
         )
 
     weight_copy = pltpu.make_async_copy(weight_hbm, weight, weight_sem)
+    bias_copy = pltpu.make_async_copy(bias_hbm, bias, bias_sem)
     for b in range(batch):
         load(0, b).start()
     weight_copy.start()
+    bias_copy.start()
     for b in range(batch):
         load(1, b).start()
 
+    sends_col = (c < 3, c > 0)
+    gets_col = (c > 0, c < 3)
+    sends_row = (r < last, r > 0)
+    gets_row = (r > 0, r < last)
+    col_to = ((c + 1) % 4, (c + 3) % 4)
+    row_to = (r + 1, r - 1)
+
     barrier = pltpu.get_barrier_semaphore()
-    for step in (1, 3):
+
+    def greet(row, col):
         pl.semaphore_signal(
-            barrier, inc=1, device_id={"rows": r, "cols": (c + step) % 4}, device_id_type=MESH
-        )
-
-    @pl.when(r > 0)
-    def _():
-        pl.semaphore_signal(barrier, inc=1, device_id={"rows": r - 1, "cols": c}, device_id_type=MESH)
-
-    @pl.when(r < last)
-    def _():
-        pl.semaphore_signal(barrier, inc=1, device_id={"rows": r + 1, "cols": c}, device_id_type=MESH)
-
-    d = lax.broadcasted_iota(jnp.int32, (2 * DISP, DISP - (DISP >> 3)), 0) % DISP
-    lane = lax.broadcasted_iota(jnp.int32, (2 * DISP, DISP - (DISP >> 3)), 1)
+            barrier, inc=1, device_id={"rows": row, "cols": col}, device_id_type=MESH
+        )
+
+    for side in range(2):
+        greet(r, col_to[side])
+        for end in range(2):
+            pl.when(jnp.logical_and(sends_col[side], sends_row[end]))(
+                functools.partial(greet, row_to[end], col_to[side])
+            )
+    for end in range(2):
+        pl.when(sends_row[end])(functools.partial(greet, row_to[end], c))
+
+    d = lax.broadcasted_iota(jnp.int32, (DISP - (DISP >> 3), 2 * DISP), 1) % DISP
+    lane = lax.broadcasted_iota(jnp.int32, (DISP - (DISP >> 3), 2 * DISP), 0)
     table = jnp.zeros(d.shape, F32)
     start = 0
     for level in range(1, LEVELS):
@@ -116,10 +128,12 @@
     @pl.when(r == 0)
     def _():
         buf[:, :, 0] = jnp.zeros((2, batch, width, channels), BF16)
+        halo_corner[:, 0] = jnp.zeros((2, 16, channels), BF16)
 
     @pl.when(r == last)
     def _():
         buf[:, :, height + 1] = jnp.zeros((2, batch, width, channels), BF16)
+        halo_corner[:, 1] = jnp.zeros((2, 16, channels), BF16)
 
     @pl.when(c == 0)
     def _():
@@ -151,7 +165,7 @@
             dst_ref=halo.at[side, image],
             send_sem=col_send.at[side, image],
             recv_sem=col_recv.at[side, image],
-            device_id={"rows": r, "cols": (c + (1 if side == 0 else 3)) % 4},
+            device_id={"rows": r, "cols": col_to[side]},
             device_id_type=MESH,
         )
 
@@ -166,20 +180,15 @@
             device_id_type=MESH,
         )
 
-    def corner_copy(side):
+    def corner_copy(side, end):
         return pltpu.make_async_remote_copy(
-            src_ref=corner.at[side],
-            dst_ref=halo_corner.at[side],
-            send_sem=corner_send.at[side],
-            recv_sem=corner_recv.at[side],
-            device_id={"rows": r, "cols": (c + (1 if side == 0 else 3)) % 4},
+            src_ref=corner.at[side, end],
+            dst_ref=halo_corner.at[side, end],
+            send_sem=corner_send.at[side, end],
+            recv_sem=corner_recv.at[side, end],
+            device_id={"rows": row_to[end], "cols": col_to[side]},
             device_id_type=MESH,
         )
-
-    sends_col = (c < 3, c > 0)
-    gets_col = (c > 0, c < 3)
-    sends_row = (r < last, r > 0)
-    gets_row = (r > 0, r < last)
 
     def each_col(conditions, action):
         for side in range(2):
@@ -195,13 +204,30 @@
                     for b in range(batch):
                         action(side, image, b)
 
+    def each_corner(col_conditions, row_conditions, action):
+        for side in range(2):
+            for end in range(2):
+                pl.when(jnp.logical_and(col_conditions[side], row_conditions[end]))(
+                    functools.partial(action, side, end)
+                )
+
     extract(0)
-    neighbours = 2 + (r > 0).astype(jnp.int32) + (r < last).astype(jnp.int32)
-    pl.semaphore_wait(barrier, neighbours)
+    beside = (c > 0).astype(jnp.int32) + (c < 3).astype(jnp.int32)
+    above = (r > 0).astype(jnp.int32) + (r < last).astype(jnp.int32)
+    pl.semaphore_wait(barrier, 2 + above + beside * above)
     each_col(sends_col, lambda side: column_copy(side, 0).start())
     each_row(sends_row, lambda side, image, b: row_copy(side, image, b).start())
     extract(1)
     each_col(sends_col, lambda side: column_copy(side, 1).start())
+    for side in range(2):
+        for end in range(2):
+            for image in range(2):
+                for b in range(batch):
+                    at = image * batch + b
+                    row = 1 if end else height
+                    corner32[side, end, at : at + 1, :] = take_column(image, b, row, side)
+            corner[side, end] = corner32[side, end].astype(BF16)
+    each_corner(sends_col, sends_row, lambda side, end: corner_copy(side, end).start())
 
     def product(image, j, slot):
         b, first, second = place(j)
@@ -223,30 +249,20 @@
                     vectors, weight[tap, 2 * side], preferred_element_type=F32
                 )
 
-    def corners_out():
-        each_row(gets_row, lambda side, image, b: row_copy(side, image, b).wait_recv())
-        for side in range(2):
-            for image in range(2):
-                for b in range(batch):
-                    for end in range(2):
-                        at = (image * batch + b) * 2 + end
-                        corner32[side, at : at + 1, :] = take_column(image, b, end * (height + 1), side)
-            corner[side] = corner32[side].astype(BF16)
-        each_col(sends_col, lambda side: corner_copy(side).start())
-
     def corners_add(image):
         for side in range(2):
             for end in range(2):
                 values = jnp.dot(
-                    halo_corner[side], weight[2 * end, 2 * side], preferred_element_type=F32
+                    halo_corner[side, end], weight[2 * end, 2 * side], preferred_element_type=F32
                 )
                 for b in range(batch):
-                    at = (image * batch + b) * 2 + end
+                    at = image * batch + b
                     to = b * 16 + end * (height + 1)
                     extra[side, 2 * end, image, to : to + 1, :] = values[at : at + 1]
 
     def corners_in():
-        each_col(gets_col, lambda side: corner_copy(side).wait_recv())
+        each_row(gets_row, lambda side, image, b: row_copy(side, image, b).wait_recv())
+        each_corner(gets_col, gets_row, lambda side, end: corner_copy(side, end).wait_recv())
         corners_add(0)
 
     column = lax.broadcasted_iota(jnp.int32, (width, channels), 0)
@@ -260,7 +276,7 @@
         before = pltpu.roll(taps[slot, 0, span, :], 1, 0)
         after = pltpu.roll(taps[slot, 2, span, :], width - 1, 0)
         total = jnp.where(column == 0, sides[0], before) + taps[slot, 1, span, :]
-        total = total + jnp.where(column == width - 1, sides[1], after) + bias_ref[...]
+        total = total + jnp.where(column == width - 1, sides[1], after) + bias[...]
         return (buf[image, b, h + 1].astype(F32) + jnp.maximum(total, 0.0)).astype(BF16)
 
     def own_copy(k, f):
@@ -307,11 +323,13 @@
             ),
         )
 
-    def relay(k):
-        b, h = place_row(k)
+    def tick(t):
+        k = t + jnp.where(c == 0, DIRECT, jnp.where(c == 3, DIRECT - LAG, 0))
+        known = jnp.clip(k, 0, rows - 1)
+        b, h = place_row(known)
         f = b * height + h
 
-        @pl.when(relays(k))
+        @pl.when(jnp.logical_and(k == known, relays(known)))
         def _():
             arrival(jnp.where(c == 3, 1, 0), f).wait_recv()
             relay_copy(f).start()
@@ -340,26 +358,26 @@
             blocks.append(pltpu.roll(scores, 1, 1, stride=1, stride_axis=0))
         lower = i1 <= i0
         volume = jnp.concatenate(
-            [jnp.where(lower, blocks[0], blocks[1]), jnp.where(lower, blocks[1], blocks[2])], axis=1
+            [
+                jnp.where(lower, blocks[0], blocks[1]).T,
+                jnp.where(lower, blocks[1], blocks[2]).T,
+            ],
+            axis=0,
         ) * (1.0 / math.sqrt(channels))
         high = volume.astype(BF16)
         low = (volume - high.astype(F32)).astype(BF16)
-        result[f, :, 0:DISP] = volume
-        result[f, :, DISP:] = jnp.dot(
-            jnp.concatenate([high, low], axis=1), pool[...], preferred_element_type=F32
-        )
-        pltpu.make_async_copy(result.at[f], out_hbm.at[b, h], out_sem.at[f]).start()
+        result[b, h, 0:DISP, :] = volume
+        result[b, h, DISP:, :] = jnp.dot(
+            pool[...], jnp.concatenate([high, low], axis=0), preferred_element_type=F32
+        )
 
     weight_copy.wait()
+    bias_copy.wait()
     product(0, 0, 0)
     from_halo(0)
 
     def right_chunk(j, _):
         slot = j % 2
-
-        @pl.when(j == 6)
-        def _():
-            corners_out()
 
         @pl.when(j == 9)
         def _():
@@ -379,13 +397,9 @@
             own_copy(2 * j, b * height + first).start()
             own_copy(2 * j + 1, b * height + second).start()
 
-        @pl.when(j == 8)
-        def _():
-            relay(0)
-
-        @pl.when(j == 11)
-        def _():
-            relay(1)
+        @pl.when(jnp.logical_or(j == 8, j == 11))
+        def _():
+            tick((j - 8) // 3)
 
         return 0
 
@@ -393,7 +407,7 @@
     from_halo(1)
     corners_add(1)
 
-    early = 6
+    early = 2 + chunks // 2
 
     def left_chunk(j, _):
         slot = (chunks + j) % 2
@@ -402,20 +416,18 @@
         for half, h in enumerate((first, second)):
             enc[1, b * height + h] = encoded(1, b, h, slot, half)
 
-        @pl.when(j % 3 == 2)
-        def _():
-            relay(2 + j // 3)
+        @pl.when(j % 2 == 1)
+        def _():
+            tick(2 + j // 2)
 
         return 0
 
     lax.fori_loop(0, chunks, left_chunk, 0)
 
     def score_row(k, _):
-        @pl.when(k + early < rows)
-        def _():
-            relay(k + early)
-
-        correlate(k)
+        tick(k + early)
+
+        correlate((k + DIRECT) % rows)
         return 0
 
     lax.fori_loop(0, rows, score_row, 0)
@@ -423,7 +435,6 @@
     def drain(k, _):
         b, h = place_row(k)
         f = b * height + h
-        pltpu.make_async_copy(result.at[f], out_hbm.at[b, h], out_sem.at[f]).wait()
 
         @pl.when(c < 3)
         def _():
@@ -437,7 +448,7 @@
 
     each_col(sends_col, lambda side: column_copy(side, 0).wait_send())
     each_col(sends_col, lambda side: column_copy(side, 1).wait_send())
-    each_col(sends_col, lambda side: corner_copy(side).wait_send())
+    each_corner(sends_col, sends_row, lambda side, end: corner_copy(side, end).wait_send())
     each_row(sends_row, lambda side, image, b: row_copy(side, image, b).wait_send())
     lax.fori_loop(0, rows, drain, 0)
 
@@ -446,46 +457,49 @@
     batch, height, width, channels = left_features.shape
     rows = batch * height
     lanes = sum(DISP >> level for level in range(LEVELS))
-    anywhere = pl.BlockSpec(memory_space=pl.ANY)
+    far = pl.BlockSpec(memory_space=pltpu.HBM)
+    near = pl.BlockSpec(memory_space=pltpu.VMEM)
     dma = pltpu.SemaphoreType.DMA
-    return pl.pallas_call(
+    arguments = (left_features, right_features, conv_weight, conv_bias.reshape(1, channels))
+    flat = pl.pallas_call(
         functools.partial(kernel, rows_total),
-        out_shape=jax.ShapeDtypeStruct((batch, height, width, lanes), F32),
-        in_specs=[anywhere, anywhere, anywhere, pl.BlockSpec(memory_space=pltpu.VMEM)],
-        out_specs=anywhere,
+        out_shape=pltpu.VMEM((batch, height, lanes, width), F32),
+        in_specs=[far] * 4,
+        out_specs=near,
         scratch_shapes=[
             pltpu.VMEM((2, batch, height + 2, width, channels), BF16),
             pltpu.VMEM((3, 3, channels, channels), BF16),
+            pltpu.VMEM((1, channels), F32),
             pltpu.VMEM((2, 3, 2 * width, channels), F32),
             pltpu.VMEM((2, rows, width, channels), BF16),
             pltpu.VMEM((2, rows, width, channels), BF16),
-            pltpu.VMEM((rows, width, lanes), F32),
-            pltpu.VMEM((2 * DISP, lanes - DISP), BF16),
+            pltpu.VMEM((lanes - DISP, 2 * DISP), BF16),
             pltpu.VMEM((width, width), BF16),
             pltpu.VMEM((2, batch, 16, channels), F32),
             pltpu.VMEM((2, 2, batch, 16, channels), BF16),
             pltpu.VMEM((2, 2, batch, 16, channels), BF16),
-            pltpu.VMEM((2, 16, channels), F32),
-            pltpu.VMEM((2, 16, channels), BF16),
-            pltpu.VMEM((2, 16, channels), BF16),
+            pltpu.VMEM((2, 2, 16, channels), F32),
+            pltpu.VMEM((2, 2, 16, channels), BF16),
+            pltpu.VMEM((2, 2, 16, channels), BF16),
             pltpu.VMEM((2, 3, 2, batch * 16, channels), F32),
             dma((2, batch)),
+            dma,
             dma,
             dma((2, 2, batch)),
             dma((2, 2, batch)),
             dma((2, 2)),
             dma((2, 2)),
-            dma((2,)),
-            dma((2,)),
+            dma((2, 2)),
+            dma((2, 2)),
             dma((rows,)),
             dma((rows,)),
             dma((2, rows)),
-            dma((rows,)),
         ],
         compiler_params=pltpu.CompilerParams(
             collective_id=0, has_side_effects=True, vmem_limit_bytes=40 * 1024 * 1024
         ),
-    )(left_features, right_features, conv_weight, conv_bias.reshape(1, channels))
+    )(*(pltpu.with_memory_space_constraint(x, pltpu.HBM) for x in arguments))
+    return jnp.swapaxes(flat, 2, 3)
 
 
 def solution(mesh):

time: 86.2 us -> 58.6 us (0.68)
  Pallas kernels: 71.1 us -> 55.2 us
  local copies, waits for them, and re-layouts: 13.8 us -> 2.58 us
    pallas_call x1, Pallas kernels: 71.1 us -> 55.2 us  [shards(): pl.pallas_call(functools.partial(kernel, rows_total), out_shape=pltpu.VME...]
    pallas_call x1 -> x0, local copies, waits for them, and re-layouts: 6.42 us -> none  [shards(): pl.pallas_call(functools.partial(kernel, rows_total), out_shape=jax.Shape...]
    unnamed x10 -> x1, local copies, waits for them, and re-layouts: 7.41 us -> 2.58 us
where the time goes in v2:
time: 58.6 us; the launch traced here: 57.8 us
  Pallas kernels  55.2 us (94%)
  local copies, waits for them, and re-layouts  2.58 us (4%)
    pallas_call x1, Pallas kernels, shards(): pl.pallas_call(functools.partial(kernel, rows_total), out_shape=pltpu.VME...  55.2 us
    unnamed x1, local copies, waits for them, and re-layouts  2.58 us

profile of v2, /device:TPU:118, one launch (start us, length us, event | category | flops | bytes accessed | tf_op | source)
XLA Modules:
  0.0 57.8 jit_solution(7190182216094305106)
XLA Ops:
  0.0 55.2 %shard_map.46 = f32[2,12,480,128]{3,2,1,0:T(8,128)S(1)} custom-call(bf16[2,12,128,256]{3,2,1,0:T(8,128)(2,1)} %left_hbm.1, bf16[2,12,128,256]{3,2,1,0:T(8,128)(2,1)} %right_hbm.1, bf16[3,3,256,256]{3,2,1,0:T(8,128)(2,1)} %weight_hbm.1, f32[1,256]{1,0:T(1,128)} %bitcast.3), custom_call_target="tpu_custom_call" | custom-call | tf_op jit(solution)/shard_map/pallas_call | solution.py:464
  55.2 2.6 %copy.6 = f32[2,12,128,480]{2,3,1,0:T(8,128)} copy(f32[2,12,128,480]{2,3,1,0:T(8,128)S(1)} %bitcast.2) | data formatting | bytes 11796480

commit v3 on v2

--- a/solution.py
+++ b/solution.py
@@ -16,6 +16,8 @@
 
 DIRECT = 2
 LAG = 3
+EARLY = (4, 5, 6, 8, 9, 10)
+PAIRED = 9
 
 
 def kernel(
@@ -73,19 +75,17 @@
         b, first, second = place(k // 2)
         return b, jnp.where(k % 2 == 0, first, second)
 
-    def load(image, b):
+    def load(image):
         return pltpu.make_async_copy(
-            images[image].at[b], buf.at[image, b, pl.ds(1, height)], load_sem.at[image, b]
+            images[image], buf.at[image, :, pl.ds(1, height)], load_sem.at[image]
         )
 
     weight_copy = pltpu.make_async_copy(weight_hbm, weight, weight_sem)
     bias_copy = pltpu.make_async_copy(bias_hbm, bias, bias_sem)
-    for b in range(batch):
-        load(0, b).start()
+    load(0).start()
     weight_copy.start()
     bias_copy.start()
-    for b in range(batch):
-        load(1, b).start()
+    load(1).start()
 
     sends_col = (c < 3, c > 0)
     gets_col = (c > 0, c < 3)
@@ -103,10 +103,6 @@
 
     for side in range(2):
         greet(r, col_to[side])
-        for end in range(2):
-            pl.when(jnp.logical_and(sends_col[side], sends_row[end]))(
-                functools.partial(greet, row_to[end], col_to[side])
-            )
     for end in range(2):
         pl.when(sends_row[end])(functools.partial(greet, row_to[end], c))
 
@@ -128,22 +124,20 @@
     @pl.when(r == 0)
     def _():
         buf[:, :, 0] = jnp.zeros((2, batch, width, channels), BF16)
-        halo_corner[:, 0] = jnp.zeros((2, 16, channels), BF16)
+        halo_corner[0] = jnp.zeros((2, 16, channels), BF16)
 
     @pl.when(r == last)
     def _():
         buf[:, :, height + 1] = jnp.zeros((2, batch, width, channels), BF16)
-        halo_corner[:, 1] = jnp.zeros((2, 16, channels), BF16)
+        halo_corner[1] = jnp.zeros((2, 16, channels), BF16)
 
     @pl.when(c == 0)
     def _():
         halo[0] = jnp.zeros(halo.shape[1:], BF16)
-        halo_corner[0] = jnp.zeros(halo_corner.shape[1:], BF16)
 
     @pl.when(c == 3)
     def _():
         halo[1] = jnp.zeros(halo.shape[1:], BF16)
-        halo_corner[1] = jnp.zeros(halo_corner.shape[1:], BF16)
 
     def take_column(image, b, row, side):
         if side == 0:
@@ -151,8 +145,7 @@
         return buf[image, b, row, 0:16, :].astype(F32)[0:1]
 
     def extract(image):
-        for b in range(batch):
-            load(image, b).wait()
+        load(image).wait()
         for side in range(2):
             for b in range(batch):
                 for h in range(height):
@@ -163,7 +156,7 @@
         return pltpu.make_async_remote_copy(
             src_ref=edge.at[side, image],
             dst_ref=halo.at[side, image],
-            send_sem=col_send.at[side, image],
+            send_sem=col_send.at[side],
             recv_sem=col_recv.at[side, image],
             device_id={"rows": r, "cols": col_to[side]},
             device_id_type=MESH,
@@ -174,19 +167,40 @@
         return pltpu.make_async_remote_copy(
             src_ref=images[image].at[b, source],
             dst_ref=buf.at[image, b, target],
-            send_sem=row_send.at[side, image, b],
-            recv_sem=row_recv.at[side, image, b],
+            send_sem=row_send.at[side],
+            recv_sem=row_recv.at[side],
             device_id={"rows": to, "cols": c},
             device_id_type=MESH,
         )
 
-    def corner_copy(side, end):
-        return pltpu.make_async_remote_copy(
-            src_ref=corner.at[side, end],
-            dst_ref=halo_corner.at[side, end],
-            send_sem=corner_send.at[side, end],
-            recv_sem=corner_recv.at[side, end],
-            device_id={"rows": row_to[end], "cols": col_to[side]},
+    def row_copies(side):
+        rows_sent = got.at[0, pl.ds(0, 2 * batch)]
+        return pltpu.make_async_remote_copy(
+            src_ref=rows_sent,
+            dst_ref=rows_sent,
+            send_sem=row_send.at[side],
+            recv_sem=row_recv.at[side],
+            device_id={"rows": row_to[side], "cols": c},
+            device_id_type=MESH,
+        )
+
+    def column_copies(side):
+        return pltpu.make_async_remote_copy(
+            src_ref=edge.at[side],
+            dst_ref=halo.at[side],
+            send_sem=col_send.at[side],
+            recv_sem=col_recv.at[side, 0],
+            device_id={"rows": r, "cols": col_to[side]},
+            device_id_type=MESH,
+        )
+
+    def corner_copy(end):
+        return pltpu.make_async_remote_copy(
+            src_ref=corner.at[end],
+            dst_ref=halo_corner.at[end],
+            send_sem=corner_send.at[end],
+            recv_sem=corner_recv.at[end],
+            device_id={"rows": row_to[end], "cols": c},
             device_id_type=MESH,
         )
 
@@ -204,31 +218,13 @@
                     for b in range(batch):
                         action(side, image, b)
 
-    def each_corner(col_conditions, row_conditions, action):
-        for side in range(2):
-            for end in range(2):
-                pl.when(jnp.logical_and(col_conditions[side], row_conditions[end]))(
-                    functools.partial(action, side, end)
-                )
-
     extract(0)
-    beside = (c > 0).astype(jnp.int32) + (c < 3).astype(jnp.int32)
     above = (r > 0).astype(jnp.int32) + (r < last).astype(jnp.int32)
-    pl.semaphore_wait(barrier, 2 + above + beside * above)
+    pl.semaphore_wait(barrier, 2 + above)
     each_col(sends_col, lambda side: column_copy(side, 0).start())
     each_row(sends_row, lambda side, image, b: row_copy(side, image, b).start())
     extract(1)
     each_col(sends_col, lambda side: column_copy(side, 1).start())
-    for side in range(2):
-        for end in range(2):
-            for image in range(2):
-                for b in range(batch):
-                    at = image * batch + b
-                    row = 1 if end else height
-                    corner32[side, end, at : at + 1, :] = take_column(image, b, row, side)
-            corner[side, end] = corner32[side, end].astype(BF16)
-    each_corner(sends_col, sends_row, lambda side, end: corner_copy(side, end).start())
-
     def product(image, j, slot):
         b, first, second = place(j)
         parts = [
@@ -241,7 +237,6 @@
             taps[slot, tap] = jnp.dot(window, matrix, preferred_element_type=F32)
 
     def from_halo(image):
-        each_col(gets_col, lambda side: column_copy(side, image).wait_recv())
         for side in range(2):
             vectors = halo[side, image].reshape(batch * 16, channels)
             for tap in range(3):
@@ -249,11 +244,24 @@
                     vectors, weight[tap, 2 * side], preferred_element_type=F32
                 )
 
+    def corners_out():
+        each_col(gets_col, lambda side: column_copy(side, 1).wait_recv())
+        for end in range(2):
+            row = 1 if end else height
+            for side in range(2):
+                for image in range(2):
+                    for b in range(batch):
+                        at = image * batch + b
+                        vector = halo[side, image, b].astype(F32)[row : row + 1]
+                        corner32[end, side, at : at + 1, :] = vector
+                corner[end, side] = corner32[end, side].astype(BF16)
+        each_col(sends_row, lambda end: corner_copy(end).start())
+
     def corners_add(image):
         for side in range(2):
             for end in range(2):
                 values = jnp.dot(
-                    halo_corner[side, end], weight[2 * end, 2 * side], preferred_element_type=F32
+                    halo_corner[end, side], weight[2 * end, 2 * side], preferred_element_type=F32
                 )
                 for b in range(batch):
                     at = image * batch + b
@@ -261,8 +269,8 @@
                     extra[side, 2 * end, image, to : to + 1, :] = values[at : at + 1]
 
     def corners_in():
-        each_row(gets_row, lambda side, image, b: row_copy(side, image, b).wait_recv())
-        each_corner(gets_col, gets_row, lambda side, end: corner_copy(side, end).wait_recv())
+        each_col(gets_row, lambda side: row_copies(side).wait_recv())
+        each_col(gets_row, lambda end: corner_copy(end).wait_recv())
         corners_add(0)
 
     column = lax.broadcasted_iota(jnp.int32, (width, channels), 0)
@@ -285,7 +293,7 @@
         return pltpu.make_async_remote_copy(
             src_ref=enc.at[0, f],
             dst_ref=got.at[0, f],
-            send_sem=own_send.at[f],
+            send_sem=own_send,
             recv_sem=got_recv.at[0, f],
             device_id={"rows": r, "cols": to},
             device_id_type=MESH,
@@ -297,7 +305,7 @@
         return pltpu.make_async_remote_copy(
             src_ref=got.at[source, f],
             dst_ref=got.at[jnp.where(c == 3, 0, 1), f],
-            send_sem=relay_send.at[f],
+            send_sem=relay_send,
             recv_sem=got_recv.at[jnp.where(c == 3, 0, 1), f],
             device_id={"rows": r, "cols": to},
             device_id_type=MESH,
@@ -307,7 +315,7 @@
         return pltpu.make_async_remote_copy(
             src_ref=got.at[which, f],
             dst_ref=got.at[which, f],
-            send_sem=relay_send.at[f],
+            send_sem=relay_send,
             recv_sem=got_recv.at[which, f],
             device_id={"rows": r, "cols": (c + 1) % 4},
             device_id_type=MESH,
@@ -334,80 +342,90 @@
             arrival(jnp.where(c == 3, 1, 0), f).wait_recv()
             relay_copy(f).start()
 
-    def correlate(k):
-        b, h = place_row(k)
-        f = b * height + h
-        direct = k < DIRECT
-
-        @pl.when(jnp.logical_or(c == 3, jnp.logical_and(c == 2, jnp.logical_not(direct))))
-        def _():
-            arrival(0, f).wait_recv()
-
-        @pl.when(jnp.logical_or(c == 2, jnp.logical_and(c == 3, direct)))
-        def _():
-            arrival(1, f).wait_recv()
-
-        query = enc[1, f]
-        blocks = []
-        for distance, keys in enumerate((enc[0, f], got[0, f], got[1, f])):
-            scores = lax.dot_general(
-                query, keys, (((1,), (1,)), ((), ())), preferred_element_type=F32
+    def correlate(steps):
+        todo = []
+        for step in steps:
+            k = (step + jnp.where(c == 2, 0, DIRECT)) % rows
+            b, h = place_row(k)
+            f = b * height + h
+            direct = k < DIRECT
+
+            @pl.when(jnp.logical_or(c == 3, jnp.logical_and(c == 2, jnp.logical_not(direct))))
+            def _(f=f):
+                arrival(0, f).wait_recv()
+
+            @pl.when(jnp.logical_or(c == 2, jnp.logical_and(c == 3, direct)))
+            def _(f=f):
+                arrival(1, f).wait_recv()
+
+            todo.append((b, h, f))
+        lower = i1 <= i0
+        for b, h, f in todo:
+            query = enc[1, f]
+            blocks = []
+            for distance, keys in enumerate((enc[0, f], got[0, f], got[1, f])):
+                scores = lax.dot_general(
+                    query, keys, (((1,), (1,)), ((), ())), preferred_element_type=F32
+                )
+                if distance:
+                    scores = jnp.where(c >= distance, scores, 0.0)
+                blocks.append(pltpu.roll(scores, 1, 1, stride=1, stride_axis=0))
+            volume = jnp.concatenate(
+                [
+                    jnp.where(lower, blocks[0], blocks[1]).T,
+                    jnp.where(lower, blocks[1], blocks[2]).T,
+                ],
+                axis=0,
+            ) * (1.0 / math.sqrt(channels))
+            high = volume.astype(BF16)
+            low = (volume - high.astype(F32)).astype(BF16)
+            result[b, h, 0:DISP, :] = volume
+            result[b, h, DISP:, :] = jnp.dot(
+                pool[...], jnp.concatenate([high, low], axis=0), preferred_element_type=F32
             )
-            if distance:
-                scores = jnp.where(c >= distance, scores, 0.0)
-            blocks.append(pltpu.roll(scores, 1, 1, stride=1, stride_axis=0))
-        lower = i1 <= i0
-        volume = jnp.concatenate(
-            [
-                jnp.where(lower, blocks[0], blocks[1]).T,
-                jnp.where(lower, blocks[1], blocks[2]).T,
-            ],
-            axis=0,
-        ) * (1.0 / math.sqrt(channels))
-        high = volume.astype(BF16)
-        low = (volume - high.astype(F32)).astype(BF16)
-        result[b, h, 0:DISP, :] = volume
-        result[b, h, DISP:, :] = jnp.dot(
-            pool[...], jnp.concatenate([high, low], axis=0), preferred_element_type=F32
-        )
 
     weight_copy.wait()
     bias_copy.wait()
     product(0, 0, 0)
+    each_col(gets_col, lambda side: column_copy(side, 0).wait_recv())
     from_halo(0)
 
-    def right_chunk(j, _):
+    def finish_right(j):
         slot = j % 2
-
-        @pl.when(j == 9)
-        def _():
-            corners_in()
-
-        following = j + 1
-        product_image = following // chunks
-        product(product_image, following % chunks, 1 - slot)
         b, first, second = place(j)
+        pair = [encoded(0, b, h, slot, half) for half, h in enumerate((first, second))]
+        turned = jnp.dot(flip[...], jnp.concatenate(pair, axis=1), preferred_element_type=F32).astype(BF16)
         for half, h in enumerate((first, second)):
-            value = encoded(0, b, h, slot, half)
-            f = b * height + h
-            enc[0, f] = jnp.dot(flip[...], value, preferred_element_type=F32).astype(BF16)
+            enc[0, b * height + h] = turned[:, half * channels : (half + 1) * channels]
 
         @pl.when(c < 3)
         def _():
             own_copy(2 * j, b * height + first).start()
             own_copy(2 * j + 1, b * height + second).start()
 
-        @pl.when(jnp.logical_or(j == 8, j == 11))
+    def right_chunk(j, _):
+        @pl.when(j == 2)
         def _():
-            tick((j - 8) // 3)
-
+            corners_out()
+
+        @pl.when(j == 9)
+        def _():
+            corners_in()
+
+        following = j + 1
+        product(following // chunks, following % chunks, 1 - j % 2)
+        finish_right(j)
+        for t, at in enumerate(EARLY):
+            pl.when(j == at)(functools.partial(tick, t))
         return 0
 
-    lax.fori_loop(0, chunks, right_chunk, 0)
+    finish_right(0)
+    product(0, 1, 1)
+    lax.fori_loop(1, chunks, right_chunk, 0)
     from_halo(1)
     corners_add(1)
 
-    early = 2 + chunks // 2
+    early = len(EARLY) + chunks // 2
 
     def left_chunk(j, _):
         slot = (chunks + j) % 2
@@ -416,41 +434,46 @@
         for half, h in enumerate((first, second)):
             enc[1, b * height + h] = encoded(1, b, h, slot, half)
 
-        @pl.when(j % 2 == 1)
+        @pl.when(j % 2 == 0)
         def _():
-            tick(2 + j // 2)
+            tick(len(EARLY) + j // 2)
 
         return 0
 
     lax.fori_loop(0, chunks, left_chunk, 0)
 
-    def score_row(k, _):
-        tick(k + early)
-
-        correlate((k + DIRECT) % rows)
+    def paired(s, _):
+        tick(early + s)
+        correlate((2 * s, 2 * s + 1))
         return 0
 
-    lax.fori_loop(0, rows, score_row, 0)
-
-    def drain(k, _):
-        b, h = place_row(k)
-        f = b * height + h
-
-        @pl.when(c < 3)
-        def _():
-            own_copy(k, f).wait_send()
-
-        @pl.when(relays(k))
-        def _():
-            relay_copy(f).wait_send()
-
+    def single(step, _):
+        tick(early - PAIRED + step)
+        correlate((step,))
         return 0
 
-    each_col(sends_col, lambda side: column_copy(side, 0).wait_send())
-    each_col(sends_col, lambda side: column_copy(side, 1).wait_send())
-    each_corner(sends_col, sends_row, lambda side, end: corner_copy(side, end).wait_send())
-    each_row(sends_row, lambda side, image, b: row_copy(side, image, b).wait_send())
-    lax.fori_loop(0, rows, drain, 0)
+    lax.fori_loop(0, PAIRED, paired, 0)
+    lax.fori_loop(2 * PAIRED, rows, single, 0)
+
+    each_col(sends_col, lambda side: column_copies(side).wait_send())
+    each_col(sends_row, lambda side: row_copies(side).wait_send())
+    each_col(sends_row, lambda end: corner_copy(end).wait_send())
+
+    def drain(sem, count):
+        rows_sent = got.at[0, pl.ds(0, count)]
+        pltpu.make_async_remote_copy(
+            src_ref=rows_sent,
+            dst_ref=rows_sent,
+            send_sem=sem,
+            recv_sem=got_recv.at[0, 0],
+            device_id={"rows": r, "cols": (c + 1) % 4},
+            device_id_type=MESH,
+        ).wait_send()
+
+    pl.when(c < 3)(lambda: drain(own_send, rows))
+    pl.when(c == 1)(lambda: drain(relay_send, rows))
+    pl.when(c == 2)(lambda: drain(relay_send, DIRECT))
+    pl.when(jnp.logical_or(c == 0, c == 3))(lambda: drain(relay_send, rows - DIRECT))
 
 
 def shards(rows_total, left_features, right_features, conv_weight, conv_bias):
@@ -482,17 +505,17 @@
             pltpu.VMEM((2, 2, 16, channels), BF16),
             pltpu.VMEM((2, 2, 16, channels), BF16),
             pltpu.VMEM((2, 3, 2, batch * 16, channels), F32),
-            dma((2, batch)),
+            dma((2,)),
             dma,
             dma,
-            dma((2, 2, batch)),
-            dma((2, 2, batch)),
+            dma((2,)),
+            dma((2,)),
+            dma((2,)),
             dma((2, 2)),
-            dma((2, 2)),
-            dma((2, 2)),
-            dma((2, 2)),
-            dma((rows,)),
-            dma((rows,)),
+            dma((2,)),
+            dma((2,)),
+            dma,
+            dma,
             dma((2, rows)),
         ],
         compiler_params=pltpu.CompilerParams(

time: 58.6 us -> 52 us (0.89); the launches traced: 57.8 us -> 51.9 us
  Pallas kernels: 55.2 us -> 49.4 us
    pallas_call x1, Pallas kernels: 55.2 us -> 49.4 us  [shards(): pl.pallas_call(functools.partial(kernel, rows_total), out_shape=pltpu.VME...]
where the time goes in v3:
time: 52 us; the launch traced here: 51.9 us
  Pallas kernels  49.4 us (95%)
  local copies, waits for them, and re-layouts  2.58 us (5%)
    pallas_call x1, Pallas kernels, shards(): pl.pallas_call(functools.partial(kernel, rows_total), out_shape=pltpu.VME...  49.4 us
    unnamed x1, local copies, waits for them, and re-layouts  2.58 us

profile of v3, /device:TPU:118, one launch (start us, length us, event | category | flops | bytes accessed | tf_op | source)
XLA Modules:
  0.0 51.9 jit_solution(4971179431836262956)
XLA Ops:
  0.0 49.4 %shard_map.46 = f32[2,12,480,128]{3,2,1,0:T(8,128)S(1)} custom-call(bf16[2,12,128,256]{3,2,1,0:T(8,128)(2,1)} %left_hbm.1, bf16[2,12,128,256]{3,2,1,0:T(8,128)(2,1)} %right_hbm.1, bf16[3,3,256,256]{3,2,1,0:T(8,128)(2,1)} %weight_hbm.1, f32[1,256]{1,0:T(1,128)} %bitcast.3), custom_call_target="tpu_custom_call" | custom-call | tf_op jit(solution)/shard_map/pallas_call | solution.py:487
  49.4 2.6 %copy.6 = f32[2,12,128,480]{2,3,1,0:T(8,128)} copy(f32[2,12,128,480]{2,3,1,0:T(8,128)S(1)} %bitcast.2) | data formatting | bytes 11796480

commit v4 on v3

--- a/solution.py
+++ b/solution.py
@@ -16,7 +16,7 @@
 
 DIRECT = 2
 LAG = 3
-EARLY = (4, 5, 6, 8, 9, 10)
+EARLY = (3, 4, 5, 7, 8, 9, 11)
 PAIRED = 9
 
 
@@ -71,6 +71,12 @@
         second = jnp.where(is_inner, 2 + 2 * (j % inner), height - 1)
         return b, first, second
 
+    def is_direct(k):
+        return jnp.logical_and(k >= DIRECT, k < 2 * DIRECT)
+
+    def round_about(u):
+        return jnp.where(u < DIRECT, u, u + DIRECT)
+
     def place_row(k):
         b, first, second = place(k // 2)
         return b, jnp.where(k % 2 == 0, first, second)
@@ -288,7 +294,7 @@
         return (buf[image, b, h + 1].astype(F32) + jnp.maximum(total, 0.0)).astype(BF16)
 
     def own_copy(k, f):
-        direct = k < DIRECT
+        direct = is_direct(k)
         to = jnp.where(c == 0, 1, jnp.where(c == 1, jnp.where(direct, 2, 0), 3))
         return pltpu.make_async_remote_copy(
             src_ref=enc.at[0, f],
@@ -322,7 +328,7 @@
         )
 
     def relays(k):
-        direct = k < DIRECT
+        direct = is_direct(k)
         return jnp.logical_or(
             c == 1,
             jnp.logical_or(
@@ -332,7 +338,7 @@
         )
 
     def tick(t):
-        k = t + jnp.where(c == 0, DIRECT, jnp.where(c == 3, DIRECT - LAG, 0))
+        k = jnp.where(c == 0, round_about(t), jnp.where(c == 3, round_about(t - LAG), t))
         known = jnp.clip(k, 0, rows - 1)
         b, h = place_row(known)
         f = b * height + h
@@ -345,10 +351,11 @@
     def correlate(steps):
         todo = []
         for step in steps:
-            k = (step + jnp.where(c == 2, 0, DIRECT)) % rows
+            late = jnp.where(step < rows - DIRECT, round_about(step), step - (rows - 2 * DIRECT))
+            k = jnp.where(c == 2, step, late)
             b, h = place_row(k)
             f = b * height + h
-            direct = k < DIRECT
+            direct = is_direct(k)
 
             @pl.when(jnp.logical_or(c == 3, jnp.logical_and(c == 2, jnp.logical_not(direct))))
             def _(f=f):

time: 52 us -> 51 us (0.981)
  Pallas kernels: 49.4 us -> 48.3 us
    pallas_call x1, Pallas kernels: 49.4 us -> 48.3 us  [shards(): pl.pallas_call(functools.partial(kernel, rows_total), out_shape=pltpu.VME...]
where the time goes in v4:
time: 51 us; the launch traced here: 50.9 us
  Pallas kernels  48.3 us (95%)
  local copies, waits for them, and re-layouts  2.58 us (5%)
    pallas_call x1, Pallas kernels, shards(): pl.pallas_call(functools.partial(kernel, rows_total), out_shape=pltpu.VME...  48.3 us
    unnamed x1, local copies, waits for them, and re-layouts  2.58 us

profile of v4, /device:TPU:118, one launch (start us, length us, event | category | flops | bytes accessed | tf_op | source)
XLA Modules:
  0.0 50.9 jit_solution(13324027623428282872)
XLA Ops:
  0.0 48.3 %shard_map.46 = f32[2,12,480,128]{3,2,1,0:T(8,128)S(1)} custom-call(bf16[2,12,128,256]{3,2,1,0:T(8,128)(2,1)} %left_hbm.1, bf16[2,12,128,256]{3,2,1,0:T(8,128)(2,1)} %right_hbm.1, bf16[3,3,256,256]{3,2,1,0:T(8,128)(2,1)} %weight_hbm.1, f32[1,256]{1,0:T(1,128)} %bitcast.3), custom_call_target="tpu_custom_call" | custom-call | tf_op jit(solution)/shard_map/pallas_call | solution.py:494
  48.3 2.6 %copy.6 = f32[2,12,128,480]{2,3,1,0:T(8,128)} copy(f32[2,12,128,480]{2,3,1,0:T(8,128)S(1)} %bitcast.2) | data formatting | bytes 11796480

commit v5 on v4

--- a/solution.py
+++ b/solution.py
@@ -293,39 +293,57 @@
         total = total + jnp.where(column == width - 1, sides[1], after) + bias[...]
         return (buf[image, b, h + 1].astype(F32) + jnp.maximum(total, 0.0)).astype(BF16)
 
-    def own_copy(k, f):
-        direct = is_direct(k)
-        to = jnp.where(c == 0, 1, jnp.where(c == 1, jnp.where(direct, 2, 0), 3))
-        return pltpu.make_async_remote_copy(
-            src_ref=enc.at[0, f],
-            dst_ref=got.at[0, f],
+    def piece(ref, which, f, part):
+        if part is None:
+            return ref.at[which, f]
+        return ref.at[which, rows - 1, pl.ds(part * (width // 2), width // 2)]
+
+    def landed(which, f, part):
+        return got_recv.at[which, f if part is None else rows - 1 + part]
+
+    def own_copy(k, f, part=None):
+        to = jnp.where(c == 0, 1, jnp.where(c == 1, jnp.where(is_direct(k), 2, 0), 3))
+        return pltpu.make_async_remote_copy(
+            src_ref=piece(enc, 0, f, part),
+            dst_ref=piece(got, 0, f, part),
             send_sem=own_send,
-            recv_sem=got_recv.at[0, f],
+            recv_sem=landed(0, f, part),
             device_id={"rows": r, "cols": to},
             device_id_type=MESH,
         )
 
-    def relay_copy(f):
+    def relay_copy(f, part=None):
         source = jnp.where(c == 3, 1, 0)
+        target = jnp.where(c == 3, 0, 1)
         to = jnp.where(c == 0, 3, jnp.where(c == 2, 3, 2))
         return pltpu.make_async_remote_copy(
-            src_ref=got.at[source, f],
-            dst_ref=got.at[jnp.where(c == 3, 0, 1), f],
+            src_ref=piece(got, source, f, part),
+            dst_ref=piece(got, target, f, part),
             send_sem=relay_send,
-            recv_sem=got_recv.at[jnp.where(c == 3, 0, 1), f],
+            recv_sem=landed(target, f, part),
             device_id={"rows": r, "cols": to},
             device_id_type=MESH,
         )
 
-    def arrival(which, f):
-        return pltpu.make_async_remote_copy(
-            src_ref=got.at[which, f],
-            dst_ref=got.at[which, f],
+    def arrival(which, f, part=None):
+        return pltpu.make_async_remote_copy(
+            src_ref=piece(got, which, f, part),
+            dst_ref=piece(got, which, f, part),
             send_sem=relay_send,
-            recv_sem=got_recv.at[which, f],
+            recv_sem=landed(which, f, part),
             device_id={"rows": r, "cols": (c + 1) % 4},
             device_id_type=MESH,
         )
+
+    def in_pieces(condition, k, f, action):
+        @pl.when(jnp.logical_and(condition, k < rows - 1))
+        def _():
+            action(f, None)
+
+        @pl.when(jnp.logical_and(condition, k == rows - 1))
+        def _():
+            for part in range(2):
+                action(f, part)
 
     def relays(k):
         direct = is_direct(k)
@@ -343,10 +361,11 @@
         b, h = place_row(known)
         f = b * height + h
 
-        @pl.when(jnp.logical_and(k == known, relays(known)))
-        def _():
-            arrival(jnp.where(c == 3, 1, 0), f).wait_recv()
-            relay_copy(f).start()
+        def action(f, part):
+            arrival(jnp.where(c == 3, 1, 0), f, part).wait_recv()
+            relay_copy(f, part).start()
+
+        in_pieces(jnp.logical_and(k == known, relays(known)), known, f, action)
 
     def correlate(steps):
         todo = []
@@ -357,14 +376,10 @@
             f = b * height + h
             direct = is_direct(k)
 
-            @pl.when(jnp.logical_or(c == 3, jnp.logical_and(c == 2, jnp.logical_not(direct))))
-            def _(f=f):
-                arrival(0, f).wait_recv()
-
-            @pl.when(jnp.logical_or(c == 2, jnp.logical_and(c == 3, direct)))
-            def _(f=f):
-                arrival(1, f).wait_recv()
-
+            near = jnp.logical_or(c == 3, jnp.logical_and(c == 2, jnp.logical_not(direct)))
+            in_pieces(near, k, f, lambda f, part: arrival(0, f, part).wait_recv())
+            distant = jnp.logical_or(c == 2, jnp.logical_and(c == 3, direct))
+            in_pieces(distant, k, f, lambda f, part: arrival(1, f, part).wait_recv())
             todo.append((b, h, f))
         lower = i1 <= i0
         for b, h, f in todo:
@@ -405,10 +420,9 @@
         for half, h in enumerate((first, second)):
             enc[0, b * height + h] = turned[:, half * channels : (half + 1) * channels]
 
-        @pl.when(c < 3)
-        def _():
-            own_copy(2 * j, b * height + first).start()
-            own_copy(2 * j + 1, b * height + second).start()
+        for half, h in enumerate((first, second)):
+            k = 2 * j + half
+            in_pieces(c < 3, k, b * height + h, lambda f, part, k=k: own_copy(k, f, part).start())
 
     def right_chunk(j, _):
         @pl.when(j == 2)
@@ -523,7 +537,7 @@
             dma((2,)),
             dma,
             dma,
-            dma((2, rows)),
+            dma((2, rows + 1)),
         ],
         compiler_params=pltpu.CompilerParams(
             collective_id=0, has_side_effects=True, vmem_limit_bytes=40 * 1024 * 1024

time: 51 us -> 50.5 us (level)
  no operation moved by 1% of the time
where the time goes in v5:
time: 50.5 us
  Pallas kernels  47.9 us (95%)
  local copies, waits for them, and re-layouts  2.58 us (5%)
    pallas_call x1, Pallas kernels, shards(): pl.pallas_call(functools.partial(kernel, rows_total), out_shape=pltpu.VME...  47.9 us
    unnamed x1, local copies, waits for them, and re-layouts  2.58 us

profile of v5, /device:TPU:118, one launch (start us, length us, event | category | flops | bytes accessed | tf_op | source)
XLA Modules:
  0.0 50.5 jit_solution(6803288676487522048)
XLA Ops:
  0.0 47.9 %shard_map.46 = f32[2,12,480,128]{3,2,1,0:T(8,128)S(1)} custom-call(bf16[2,12,128,256]{3,2,1,0:T(8,128)(2,1)} %left_hbm.1, bf16[2,12,128,256]{3,2,1,0:T(8,128)(2,1)} %right_hbm.1, bf16[3,3,256,256]{3,2,1,0:T(8,128)(2,1)} %weight_hbm.1, f32[1,256]{1,0:T(1,128)} %bitcast.3), custom_call_target="tpu_custom_call" | custom-call | tf_op jit(solution)/shard_map/pallas_call | solution.py:508
  47.9 2.6 %copy.6 = f32[2,12,128,480]{2,3,1,0:T(8,128)} copy(f32[2,12,128,480]{2,3,1,0:T(8,128)S(1)} %bitcast.2) | data formatting | bytes 11796480

commit v6 on v5

--- a/solution.py
+++ b/solution.py
@@ -88,10 +88,6 @@
 
     weight_copy = pltpu.make_async_copy(weight_hbm, weight, weight_sem)
     bias_copy = pltpu.make_async_copy(bias_hbm, bias, bias_sem)
-    load(0).start()
-    weight_copy.start()
-    bias_copy.start()
-    load(1).start()
 
     sends_col = (c < 3, c > 0)
     gets_col = (c > 0, c < 3)
@@ -111,6 +107,11 @@
         greet(r, col_to[side])
     for end in range(2):
         pl.when(sends_row[end])(functools.partial(greet, row_to[end], c))
+
+    load(0).start()
+    weight_copy.start()
+    bias_copy.start()
+    load(1).start()
 
     d = lax.broadcasted_iota(jnp.int32, (DISP - (DISP >> 3), 2 * DISP), 1) % DISP
     lane = lax.broadcasted_iota(jnp.int32, (DISP - (DISP >> 3), 2 * DISP), 0)

time: 50.5 us -> 50.5 us (level)
  no operation moved by 1% of the time
where the time goes in v6:
time: 50.5 us
  Pallas kernels  47.9 us (95%)
  local copies, waits for them, and re-layouts  2.58 us (5%)
    pallas_call x1, Pallas kernels, shards(): pl.pallas_call(functools.partial(kernel, rows_total), out_shape=pltpu.VME...  47.9 us
    unnamed x1, local copies, waits for them, and re-layouts  2.58 us

profile of v6, /device:TPU:118, one launch (start us, length us, event | category | flops | bytes accessed | tf_op | source)
XLA Modules:
  0.0 50.5 jit_solution(17193897070299645028)
XLA Ops:
  0.0 47.9 %shard_map.46 = f32[2,12,480,128]{3,2,1,0:T(8,128)S(1)} custom-call(bf16[2,12,128,256]{3,2,1,0:T(8,128)(2,1)} %left_hbm.1, bf16[2,12,128,256]{3,2,1,0:T(8,128)(2,1)} %right_hbm.1, bf16[3,3,256,256]{3,2,1,0:T(8,128)(2,1)} %weight_hbm.1, f32[1,256]{1,0:T(1,128)} %bitcast.3), custom_call_target="tpu_custom_call" | custom-call | tf_op jit(solution)/shard_map/pallas_call | solution.py:509
  47.9 2.6 %copy.6 = f32[2,12,128,480]{2,3,1,0:T(8,128)} copy(f32[2,12,128,480]{2,3,1,0:T(8,128)S(1)} %bitcast.2) | data formatting | bytes 11796480
